TPU v7x, 256 devices: a whole 4x4x8 slice. The times are simulated.
256 devices in a mesh: engine: 4 (over y), ep: 64 (over x, z, core).
Axes of the slice: x: 4, y: 4, z: 8, core: 2. Of those that a mesh axis runs over, the one named last changes fastest.
Arguments:
- tokens: bfloat16 [2, 2048, 4096], P(None, ('engine', 'ep')), may hold values from -6 to 6
- route_ids: int32 [2, 2048, 8], P(None, ('engine', 'ep')), may hold values from 0 to 63, all different within a row; in each aligned block of 8 rows (0 to 7, 8 to 15, ..., all dimensions but the last counted through in order) at most 2 rows name the same one
- route_weights: float32 [2, 2048, 8], P(None, ('engine', 'ep')), may hold values from 0.05 to 1
- placement: int32 [64], replicated, may hold values from 0 to 63, each once
- expert_in: bfloat16 [64, 2, 4096, 1536], P(None, None, ('engine', 'ep')), may hold values from -0.09375 to 0.09375
- expert_down: bfloat16 [64, 1536, 4096], P(None, None, ('engine', 'ep')), may hold values from -0.15625 to 0.15625
Outputs:
- combined: bfloat16 [2, 2048, 4096], P(None, ('engine', 'ep'))
- in_scales: float32 [64, 2, 1536], P('ep', None, 'engine')
- out_scales: float32 [64, 4096], P('ep', 'engine')
Inputs may be any that keep to these rules, and one draw needn't show every extreme that they name: `route_ids`: within the rows of one device in one step no expert is named more than 2 times, a bound that some block reaches. `placement`: each slot holds exactly one expert.
All inputs are finite; a program needn't handle non-finite values.
Results may differ from a plain program's by a relative error of at most 0.0057.
Values may be sent and summed in bfloat16 or wider, within the bound.
A program may use at most 128 MiB of HBM per device.

v0:
```python
import jax
import jax.numpy as jnp
from jax import lax
from jax.sharding import PartitionSpec as P

EPSILON = 1e-06
quant_levels = 31.0


def in_blocks(shard, dim, peers):
    lengths = shard.shape
    parts = shard.reshape(*lengths[:dim], peers, lengths[dim] // peers, *lengths[dim + 1 :])
    return jnp.moveaxis(parts, dim, 0)


def in_order(parts, dim):
    lengths = list(parts.shape[1:])
    lengths[dim] *= parts.shape[0]
    return jnp.moveaxis(parts, 0, dim).reshape(lengths)


def one_exchange(shard, axis, axes, splits, concats):
    sizes = [lax.axis_size(a) for a in axes]
    parts = in_blocks(shard, splits[0], sizes[0])
    parts = jnp.moveaxis(in_blocks(parts, splits[1] + 1, sizes[1]), 0, 1)
    inside = parts.shape[2:]
    parts = parts.reshape(-1, *inside)
    parts = lax.all_to_all(parts, axis, split_axis=0, concat_axis=0, tiled=True)
    parts = in_order(parts.reshape(*sizes, *inside), concats[0] + 1)
    return in_order(parts, concats[1])


def slot_targets(picked, placement, capacity):
    experts = placement.shape[0]
    numbers = jnp.arange(experts, dtype=jnp.int32)
    slot_ids = jnp.sum(jnp.where(picked[..., None] == numbers, placement, 0), axis=-1)
    flat_slots = slot_ids.reshape(-1)
    marked = (flat_slots[:, None] == numbers[None, :]).astype(jnp.int32)
    before = jnp.cumsum(marked, axis=0) - marked
    positions = jnp.sum(before * marked, axis=1)
    return (flat_slots * capacity + positions).reshape(slot_ids.shape)


def pack_rows(local_rows, targets, lane_count):
    lane_ids = jnp.arange(lane_count, dtype=jnp.int32)
    selector = jnp.sum((targets[None, :, :] == lane_ids[:, None, None]).astype(jnp.int32), axis=2)
    return jnp.dot(
        selector.astype(jnp.bfloat16), local_rows, preferred_element_type=jnp.float32
    ).astype(jnp.bfloat16)


def shards(tokens, route_ids, route_weights, placement, expert_in, expert_down):
    experts = placement.shape[0]
    numbers = jnp.arange(experts, dtype=jnp.int32)
    owners = jnp.sum(jnp.where(placement[None, :] == numbers[:, None], numbers[None, :], 0), axis=1)
    sorted_in = jnp.take(expert_in, owners, axis=0)
    sorted_down = jnp.take(expert_down, owners, axis=0)
    engines = lax.axis_size("engine")
    peer_count = lax.axis_size("ep")
    quarter_in, held_down = (
        lax.all_to_all(sorted_in, "ep", split_axis=0, concat_axis=2, tiled=True),
        lax.all_to_all(sorted_down, "ep", split_axis=0, concat_axis=2, tiled=True),
    )
    held_in = lax.all_to_all(quarter_in, "engine", split_axis=3, concat_axis=2, tiled=True)
    scale_in = (jnp.max(jnp.abs(held_in.astype(jnp.float32)), axis=2) + EPSILON) / quant_levels
    quant_in = jnp.floor(held_in.astype(jnp.float32) / scale_in[:, :, None, :] + 0.5).astype(
        jnp.bfloat16
    )
    scale_out = (jnp.max(jnp.abs(held_down.astype(jnp.float32)), axis=1) + EPSILON) / quant_levels
    quant_down = jnp.floor(held_down.astype(jnp.float32) / scale_out[:, None, :] + 0.5).astype(
        jnp.bfloat16
    )
    held_count = quant_in.shape[0]
    row_count = tokens.shape[1]
    top_count = route_ids.shape[2]
    capacity = max(2, (row_count * top_count + experts - 1) // experts)
    lane_count = experts * capacity
    results = []
    for step_index in range(tokens.shape[0]):
        local_rows = tokens[step_index]
        picked = route_ids[step_index]
        targets = slot_targets(picked, placement, capacity)
        packed = pack_rows(local_rows, targets, lane_count).reshape(experts, capacity, -1)
        arrived = lax.all_to_all(packed, "ep", split_axis=0, concat_axis=1, tiled=True)
        arrived = arrived.reshape(held_count, peer_count, capacity, -1)
        projected = jnp.einsum(
            "xpnd,xmdf->xmpnf",
            lax.all_gather(arrived, "engine", axis=2, tiled=True),
            quant_in,
            preferred_element_type=jnp.float32,
        )
        projected = projected * scale_in[:, :, None, None, :]
        hidden = (jax.nn.silu(projected[:, 0]) * projected[:, 1]).astype(jnp.bfloat16)
        summed = jnp.einsum(
            "xpcj,xjd->xpcd",
            lax.all_gather(hidden, "engine", axis=3, tiled=True),
            quant_down,
            preferred_element_type=jnp.float32,
        )
        outcome = (summed * scale_out[:, None, None, :]).astype(jnp.bfloat16)
        outcome = outcome.reshape(held_count, peer_count, engines, capacity, -1)
        returned = one_exchange(outcome, ("engine", "ep"), ("engine", "ep"), (2, 1), (4, 0))
        returned = returned.reshape(lane_count, -1)
        lane_ids = jnp.arange(lane_count, dtype=jnp.int32)
        mixing = jnp.sum(
            jnp.where(targets[:, :, None] == lane_ids, route_weights[step_index][:, :, None], 0.0),
            axis=1,
        )
        merged = jnp.dot(mixing, returned.astype(jnp.float32), precision=lax.Precision.HIGHEST)
        results.append(merged.astype(jnp.bfloat16))
    return (jnp.stack(results), scale_in, scale_out)


def solution(mesh):
    placed = (
        P(None, ("engine", "ep"), None),
        P(None, ("engine", "ep"), None),
        P(None, ("engine", "ep"), None),
        P(),
        P(None, None, ("engine", "ep"), None),
        P(None, None, ("engine", "ep")),
    )
    return jax.shard_map(
        shards,
        mesh=mesh,
        in_specs=placed,
        out_specs=(P(None, ("engine", "ep"), None), P("ep", None, "engine"), P("ep", "engine")),
        check_vma=False,
    )
```

profile of v0, /device:TPU:1, one launch (start us, length us, event | category | flops | bytes accessed | tf_op | source)
XLA Modules:
  0.0 534.4 jit_solution(12656317761184367620)
XLA Ops:
  12.2 2.5 reshape.356
  14.8 13.2 %all-to-all-start.5 = ((bf16[64,2,4096]{2,1,0:T(2,128)(2,1)}), bf16[64,2,4096]{2,1,0:T(2,128)(2,1)}, u32[]{:S(2)}, u32[]{:S(2)}) async-start(bf16[64,2,4096]{2,1,0:T(2,128)(2,1)} %reshape.356), calls=%async_computation.5 | async-start | bytes 2097152 | tf_op jit(solution)/shard_map/all_to_all | solution.py:84
  28.1 6.4 %gather_fusion = bf16[64,2,16,1536]{3,2,1,0:T(8,128)(2,1)} fusion(bf16[64,2,16,1536]{3,2,1,0:T(8,128)(2,1)} %param.10, s32[1024]{0:T(1024)S(1)} %pad_clamp_fusion), kind=kCustom, calls=%fused_computation | custom fusion | bytes 12583168 | tf_op jit(solution)/shard_map/jit(_take)/gather | solution.py:56
  34.5 6.1 %broadcast_select_fusion = bf16[64,2,16,1536]{3,2,1,0:T(8,128)(2,1)} fusion(bf16[64,2,16,1536]{3,2,1,0:T(8,128)(2,1)} %gather_fusion, pred[64]{0:T(512)(128)(4,1)S(1)} %compare_and_fusion), kind=kLoop, calls=%fused_computation.15 | loop fusion | flops 3145728 | bytes 12582976 | tf_op jit(solution)/shard_map/jit(_take)/select_n | solution.py:56
  40.6 15.8 %all-to-all-done.5 = bf16[64,2,4096]{2,1,0:T(2,128)(2,1)} async-done(((bf16[64,2,4096]{2,1,0:T(2,128)(2,1)}), bf16[64,2,4096]{2,1,0:T(2,128)(2,1)}, u32[]{:S(2)}, u32[]{:S(2)}) %all-to-all-start.5) | async-done | bytes 1048608 | tf_op jit(solution)/shard_map/all_to_all | solution.py:84
  56.4 6.4 %all-to-all-start = ((bf16[64,2,16,1536]{3,2,1,0:T(8,128)(2,1)}), bf16[64,2,16,1536]{3,2,1,0:T(8,128)(2,1)}, u32[]{:S(2)}, u32[]{:S(2)}) async-start(bf16[64,2,16,1536]{3,2,1,0:T(8,128)(2,1)} %broadcast_select_fusion), calls=%async_computation | async-start | bytes 12582912 | tf_op jit(solution)/shard_map/all_to_all | solution.py:61
  63.4 2.8 copy.65
  67.7 2.6 reshape.351
  70.3 133.3 %all-to-all-done = bf16[64,2,16,1536]{3,2,1,0:T(8,128)(2,1)} async-done(((bf16[64,2,16,1536]{3,2,1,0:T(8,128)(2,1)}), bf16[64,2,16,1536]{3,2,1,0:T(8,128)(2,1)}, u32[]{:S(2)}, u32[]{:S(2)}) %all-to-all-start) | async-done | bytes 6291488 | tf_op jit(solution)/shard_map/all_to_all | solution.py:61
  203.6 6.0 %all-to-all-start.2 = ((bf16[64,2,4096]{2,1,0:T(2,128)(2,1)}), bf16[64,2,4096]{2,1,0:T(2,128)(2,1)}, u32[]{:S(2)}, u32[]{:S(2)}) async-start(bf16[64,2,4096]{2,1,0:T(2,128)(2,1)} %reshape.351), calls=%async_computation.2 | async-start | bytes 2097152 | tf_op jit(solution)/shard_map/all_to_all | solution.py:84
  209.5 6.0 %copy.55 = bf16[1,2,64,16,1536]{4,3,2,1,0:T(8,128)(2,1)} copy(bf16[1,2,64,16,1536]{4,3,1,2,0:T(8,128)(2,1)} %bitcast.5) | data formatting | bytes 12582912 | tf_op jit(solution)/shard_map/all_to_all | solution.py:61
  215.5 16.4 %copy.56 = bf16[1,2,1024,1536]{2,1,0,3:T(2,128)(2,1)} copy(bf16[1,2,1024,1536]{3,2,1,0:T(8,128)(2,1)} %bitcast.119) | data formatting | bytes 12582912 | tf_op jit(solution)/shard_map/all_to_all | solution.py:61
  231.9 6.1 %all-to-all-done.2 = bf16[64,2,4096]{2,1,0:T(2,128)(2,1)} async-done(((bf16[64,2,4096]{2,1,0:T(2,128)(2,1)}), bf16[64,2,4096]{2,1,0:T(2,128)(2,1)}, u32[]{:S(2)}, u32[]{:S(2)}) %all-to-all-start.2) | async-done | bytes 1048608 | tf_op jit(solution)/shard_map/all_to_all | solution.py:84
  238.0 5.2 all-to-all-start.1
  243.3 2.4 gather_fusion.1
  245.7 3.0 copy.59
  250.8 97.5 %all-to-all-done.1 = bf16[1,2,1024,1536]{2,1,0,3:T(2,128)(2,1)} async-done(((bf16[1,2,1024,1536]{2,1,0,3:T(2,128)(2,1)}), bf16[1,2,1024,1536]{2,1,0,3:T(2,128)(2,1)}, u32[]{:S(2)}, u32[]{:S(2)}) %all-to-all-start.1) | async-done | bytes 6291488 | tf_op jit(solution)/shard_map/all_to_all | solution.py:64
  348.3 6.6 %all-to-all-start.3 = ((bf16[64,1536,16]{1,2,0:T(8,128)(2,1)}), bf16[64,1536,16]{1,2,0:T(8,128)(2,1)S(1)}, u32[]{:S(2)}, u32[]{:S(2)}) async-start(bf16[64,1536,16]{1,2,0:T(8,128)(2,1)} %broadcast_select_fusion.1), calls=%async_computation.3 | async-start | bytes 6291456 | tf_op jit(solution)/shard_map/all_to_all | solution.py:62
  355.1 4.8 copy.57
  362.1 4.2 fusion.8
  366.3 8.7 %copy.58 = bf16[1,2,4,1024,384]{4,3,2,1,0:T(8,128)(2,1)} copy(bf16[1,2,4,1024,384]{3,4,2,1,0:T(8,128)(2,1)} %fusion.8) | data formatting | bytes 12582912 | tf_op jit(solution)/shard_map/floor | solution.py:66
  374.9 7.1 %fusion.15 = f32[1,2,64,8,384]{4,2,3,1,0:T(8,128)S(1)} fusion(bf16[2,4096,384,1]{2,1,3,0:T(8,128)(2,1)} %bitcast.120, bf16[64,8,4096]{2,0,1:T(8,128)(2,1)} %all-gather.13.cloned.1.call-done, f32[2,384]{1,0:T(2,128)S(1)} %get-tuple-element.10), kind=kOutput, calls=%fused_computation.30 | convolution fusion | flops 3221618688 | bytes 12061696 | tf_op jit(solution)/shard_map/xpnd,xmdf->xmpnf/dot_general | solution.py:86
  383.3 45.0 %all-to-all-done.3 = bf16[64,1536,16]{1,2,0:T(8,128)(2,1)S(1)} async-done(((bf16[64,1536,16]{1,2,0:T(8,128)(2,1)}), bf16[64,1536,16]{1,2,0:T(8,128)(2,1)S(1)}, u32[]{:S(2)}, u32[]{:S(2)}) %all-to-all-start.3) | async-done | bytes 3145760 | tf_op jit(solution)/shard_map/all_to_all | solution.py:62
  429.0 7.1 %fusion.16 = f32[1,2,64,8,384]{4,2,3,1,0:T(8,128)S(1)} fusion(bf16[2,4096,384,1]{2,1,3,0:T(8,128)(2,1)} %bitcast.121, bf16[64,8,4096]{2,0,1:T(8,128)(2,1)} %all-gather.11.cloned.1.call-done, f32[2,384]{1,0:T(2,128)S(1)} %get-tuple-element.10), kind=kOutput, calls=%fused_computation.32 | convolution fusion | flops 3221618688 | bytes 12061696 | tf_op jit(solution)/shard_map/xpnd,xmdf->xmpnf/dot_general | solution.py:86
  439.6 4.4 multiply_convert_fusion
  447.1 6.4 %all-to-all-start.6 = ((bf16[256,1,1,1,2,1024]{5,4,3,2,1,0:T(2,128)(2,1)}), bf16[256,1,1,1,2,1024]{5,4,3,2,1,0:T(2,128)(2,1)S(1)}, u32[]{:S(2)}, u32[]{:S(2)}) async-start(bf16[256,1,1,1,2,1024]{5,4,3,2,1,0:T(2,128)(2,1)} %copy.69), calls=%async_computation.6 | async-start | bytes 2097152 | tf_op jit(solution)/shard_map/all_to_all | solution.py:28
  453.5 9.7 %all-gather.7.cloned.1.call-done = bf16[1,64,8,1536]{3,1,2,0:T(8,128)(2,1)} async-done(((bf16[1,64,8,384]{3,1,2,0:T(8,128)(2,1)}), bf16[1,64,8,1536]{3,1,2,0:T(8,128)(2,1)}) %all-gather.7.cloned.1.call-update) | async-done | bytes 1572880 | tf_op jit(solution)/shard_map/all_gather | solution.py:96
  463.2 4.4 multiply_convert_fusion.1
  470.7 15.3 %all-to-all-done.6 = bf16[256,1,1,1,2,1024]{5,4,3,2,1,0:T(2,128)(2,1)S(1)} async-done(((bf16[256,1,1,1,2,1024]{5,4,3,2,1,0:T(2,128)(2,1)}), bf16[256,1,1,1,2,1024]{5,4,3,2,1,0:T(2,128)(2,1)S(1)}, u32[]{:S(2)}, u32[]{:S(2)}) %all-to-all-start.6) | async-done | bytes 1048608 | tf_op jit(solution)/shard_map/all_to_all | solution.py:28
  485.9 6.8 %all-to-all-start.4 = ((bf16[256,1,1,1,2,1024]{5,4,3,2,1,0:T(2,128)(2,1)}), bf16[256,1,1,1,2,1024]{5,4,3,2,1,0:T(2,128)(2,1)}, u32[]{:S(2)}, u32[]{:S(2)}) async-start(bf16[256,1,1,1,2,1024]{5,4,3,2,1,0:T(2,128)(2,1)} %copy.63), calls=%async_computation.4 | async-start | bytes 2097152 | tf_op jit(solution)/shard_map/all_to_all | solution.py:28
  496.3 26.8 %all-to-all-done.4 = bf16[256,1,1,1,2,1024]{5,4,3,2,1,0:T(2,128)(2,1)} async-done(((bf16[256,1,1,1,2,1024]{5,4,3,2,1,0:T(2,128)(2,1)}), bf16[256,1,1,1,2,1024]{5,4,3,2,1,0:T(2,128)(2,1)}, u32[]{:S(2)}, u32[]{:S(2)}) %all-to-all-start.4) | async-done | bytes 1048608 | tf_op jit(solution)/shard_map/all_to_all | solution.py:28
  523.1 2.7 copy.64
  (71 shorter events, 29.0 us)
Async XLA Ops:
  7.2 236.1 %copy-start = (bf16[64,1536,16]{1,2,0:T(8,128)(2,1)S(1)}, bf16[64,1536,16]{1,2,0:T(8,128)(2,1)}, u32[]{:S(2)}) copy-start(bf16[64,1536,16]{1,2,0:T(8,128)(2,1)} %param.11) | copy-start | bytes 9437188
  7.2 20.8 %copy-start.6 = (s32[64]{0:T(128)S(1)}, s32[64]{0:T(128)}, u32[]{:S(2)}) copy-start(s32[64]{0:T(128)} %param.9) | copy-start | bytes 772
  14.8 41.6 %all-to-all-start.5 = ((bf16[64,2,4096]{2,1,0:T(2,128)(2,1)}), bf16[64,2,4096]{2,1,0:T(2,128)(2,1)}, u32[]{:S(2)}, u32[]{:S(2)}) async-start(bf16[64,2,4096]{2,1,0:T(2,128)(2,1)} %reshape.356), calls=%async_computation.5 | async-start | bytes 2097152 | tf_op jit(solution)/shard_map/all_to_all | solution.py:84
  40.6 25.7 %copy-start.4 = (bf16[2,8,4096]{2,1,0:T(8,128)(2,1)S(1)}, bf16[2,8,4096]{2,1,0:T(8,128)(2,1)}, u32[]{:S(2)}) copy-start(bf16[2,8,4096]{2,1,0:T(8,128)(2,1)} %param.6) | copy-start | bytes 393220
  56.4 147.2 %all-to-all-start = ((bf16[64,2,16,1536]{3,2,1,0:T(8,128)(2,1)}), bf16[64,2,16,1536]{3,2,1,0:T(8,128)(2,1)}, u32[]{:S(2)}, u32[]{:S(2)}) async-start(bf16[64,2,16,1536]{3,2,1,0:T(8,128)(2,1)} %broadcast_select_fusion), calls=%async_computation | async-start | bytes 12582912 | tf_op jit(solution)/shard_map/all_to_all | solution.py:61
  62.7 312.2 %all-gather.13.cloned.1.call-start = ((), (), s32[]{:S(2)}) async-start(), calls=%async_computation.10 | async-start | bytes 5242880 | tf_op jit(solution)/shard_map/all_gather | solution.py:88
  203.6 34.4 %all-to-all-start.2 = ((bf16[64,2,4096]{2,1,0:T(2,128)(2,1)}), bf16[64,2,4096]{2,1,0:T(2,128)(2,1)}, u32[]{:S(2)}, u32[]{:S(2)}) async-start(bf16[64,2,4096]{2,1,0:T(2,128)(2,1)} %reshape.351), calls=%async_computation.2 | async-start | bytes 2097152 | tf_op jit(solution)/shard_map/all_to_all | solution.py:84
  238.0 110.3 %all-to-all-start.1 = ((bf16[1,2,1024,1536]{2,1,0,3:T(2,128)(2,1)}), bf16[1,2,1024,1536]{2,1,0,3:T(2,128)(2,1)}, u32[]{:S(2)}, u32[]{:S(2)}) async-start(bf16[1,2,1024,1536]{2,1,0,3:T(2,128)(2,1)} %copy.56), calls=%async_computation.1 | async-start | bytes 12582912 | tf_op jit(solution)/shard_map/all_to_all | solution.py:64
  243.2 185.8 %all-gather.11.cloned.1.call-start = ((), (), s32[]{:S(2)}) async-start(), calls=%async_computation.9 | async-start | bytes 5242880 | tf_op jit(solution)/shard_map/all_gather | solution.py:88
  245.7 3.1 copy-start.2
  348.3 80.0 %all-to-all-start.3 = ((bf16[64,1536,16]{1,2,0:T(8,128)(2,1)}), bf16[64,1536,16]{1,2,0:T(8,128)(2,1)S(1)}, u32[]{:S(2)}, u32[]{:S(2)}) async-start(bf16[64,1536,16]{1,2,0:T(8,128)(2,1)} %broadcast_select_fusion.1), calls=%async_computation.3 | async-start | bytes 6291456 | tf_op jit(solution)/shard_map/all_to_all | solution.py:62
  354.9 84.8 %all-gather.9.cloned.1.call-start = ((), (), s32[]{:S(2)}) async-start(), calls=%async_computation.8 | async-start | bytes 1966080 | tf_op jit(solution)/shard_map/all_gather | solution.py:96
  383.1 80.2 %all-gather.7.cloned.1.call-start = ((), (), s32[]{:S(2)}) async-start(), calls=%async_computation.7 | async-start | bytes 1966080 | tf_op jit(solution)/shard_map/all_gather | solution.py:96
  447.1 38.8 %all-to-all-start.6 = ((bf16[256,1,1,1,2,1024]{5,4,3,2,1,0:T(2,128)(2,1)}), bf16[256,1,1,1,2,1024]{5,4,3,2,1,0:T(2,128)(2,1)S(1)}, u32[]{:S(2)}, u32[]{:S(2)}) async-start(bf16[256,1,1,1,2,1024]{5,4,3,2,1,0:T(2,128)(2,1)} %copy.69), calls=%async_computation.6 | async-start | bytes 2097152 | tf_op jit(solution)/shard_map/all_to_all | solution.py:28
  467.6 25.2 %copy-start.5 = (f32[2,8,8]{2,1,0:T(8,128)S(1)}, f32[2,8,8]{2,1,0:T(8,128)}, u32[]{:S(2)}) copy-start(f32[2,8,8]{2,1,0:T(8,128)} %param.8) | copy-start | bytes 1540
  485.9 37.2 %all-to-all-start.4 = ((bf16[256,1,1,1,2,1024]{5,4,3,2,1,0:T(2,128)(2,1)}), bf16[256,1,1,1,2,1024]{5,4,3,2,1,0:T(2,128)(2,1)}, u32[]{:S(2)}, u32[]{:S(2)}) async-start(bf16[256,1,1,1,2,1024]{5,4,3,2,1,0:T(2,128)(2,1)} %copy.63), calls=%async_computation.4 | async-start | bytes 2097152 | tf_op jit(solution)/shard_map/all_to_all | solution.py:28
  495.0 32.9 %copy-start.1 = (bf16[64,1536,16]{1,2,0:T(8,128)(2,1)S(1)}, bf16[64,1536,16]{1,2,0:T(8,128)(2,1)}, u32[]{:S(2)}) copy-start(bf16[64,1536,16]{1,2,0:T(8,128)(2,1)} %param.11) | copy-start | bytes 9437188
  523.1 3.1 copy-start.3
Sparse Core Ops, SparseCore 0:
  66.4 51.7 all-gather.12
  248.9 81.6 all-gather.10
  383.2 27.9 all-gather.8
  437.3 25.8 all-gather.6
where the time goes:
time: 536 us; the launch traced here: 534 us
  waiting for transfers between devices  349 us (65%)
  local copies, waits for them, and re-layouts  69.4 us (13%)
  starting transfers between devices  51.1 us (10%)
  matrix products  27.8 us (5%)
  other arithmetic  22.6 us (4%)
  between operations  14.1 us (3%)
    all_to_all x1, waiting for transfers between devices, shards(): lax.all_to_all(sorted_in, 'ep', split_axis=0, concat_axis=2, tiled=True)  133 us
    all_to_all x1, waiting for transfers between devices, shards(): lax.all_to_all(quarter_in, 'engine', split_axis=3, concat_axis=2, tiled=T...  97.5 us
    all_to_all x1, waiting for transfers between devices, shards(): lax.all_to_all(sorted_down, 'ep', split_axis=0, concat_axis=2, tiled=True)  45 us
    all_to_all x2, waiting for transfers between devices, one_exchange(): parts = lax.all_to_all(parts, axis, split_axis=0, concat_axis=0, tiled=True)  42 us
    all_to_all x2, local copies, waits for them, and re-layouts, shards(): lax.all_to_all(sorted_in, 'ep', split_axis=0, concat_axis=2, tiled=True)  22.3 us
    all_to_all x2, waiting for transfers between devices, shards(): lax.all_to_all(packed, 'ep', split_axis=0, concat_axis=1, tiled=True)  21.9 us
    all_to_all x2, starting transfers between devices, shards(): lax.all_to_all(packed, 'ep', split_axis=0, concat_axis=1, tiled=True)  19.1 us
    dot_general x2, matrix products, shards(): jnp.einsum('xpnd,xmdf->xmpnf', lax.all_gather(arrived, 'engine', axis=2,...  14.2 us
  transfers between devices with their start and end apart: 11, of which 8 were waited for; matrix products, arithmetic and copies ran while one was open for 20% of the time, Pallas kernels for 0%

commit v1 on v0

v1 whole, which is shorter than its diff:
```python
import jax
import jax.numpy as jnp
from jax import lax
from jax.sharding import PartitionSpec as P

EPSILON = 1e-06
quant_levels = 31.0
BOTH = ("engine", "ep")


def first_slots(named, capacity):
    counted = named.astype(jnp.int32)
    before = jnp.cumsum(counted, axis=-2) - counted
    return jnp.stack([named & (before == slot) for slot in range(capacity)], axis=-3)


def shards(tokens, route_ids, route_weights, placement, expert_in, expert_down):
    experts = placement.shape[0]
    engines = lax.axis_size("engine")
    peers = lax.axis_size("ep")
    me = lax.axis_index("ep")
    steps, row_count, width = tokens.shape
    capacity = 2
    hidden_units = expert_in.shape[3]
    units = hidden_units // engines
    shard_rows = expert_in.shape[2]
    numbers = jnp.arange(experts, dtype=jnp.int32)
    mine = jnp.sum(jnp.where(placement == me, numbers, 0))

    ids = jnp.pad(route_ids, ((0, 0), (0, 0), (0, 128 - route_ids.shape[2])), constant_values=-1)
    payload = jnp.concatenate([tokens, ids.astype(jnp.bfloat16)], axis=2)
    everyone = lax.all_gather(payload, "ep", axis=0, tiled=False)

    parts = jnp.concatenate([expert_in[..., e * units : (e + 1) * units] for e in range(engines)], axis=0)
    held_in = lax.all_to_all(parts, BOTH, split_axis=0, concat_axis=0, tiled=True)

    down = jnp.transpose(expert_down, (0, 2, 1))
    down_top = jnp.max(jnp.abs(down), axis=2).astype(jnp.float32)
    down_scale = (down_top + EPSILON) / quant_levels
    quant_down = jnp.floor(down.astype(jnp.float32) / down_scale[:, :, None] + 0.5).astype(jnp.bfloat16)
    all_down_scales = lax.all_gather(down_scale, "ep", axis=1, tiled=True)
    held_down = lax.all_to_all(quant_down, "ep", split_axis=0, concat_axis=0, tiled=True)
    scale_out = lax.dynamic_index_in_dim(all_down_scales, me, 0, keepdims=False)
    out_scales = lax.dynamic_index_in_dim(all_down_scales, mine, 0, keepdims=True)

    named = jnp.any(everyone[..., width : width + route_ids.shape[2]] == me.astype(jnp.bfloat16), axis=-1)
    slots = first_slots(named[..., None], capacity)[..., 0]
    same = jnp.eye(peers, dtype=jnp.bool_)
    arrived = []
    for step in range(steps):
        chosen = (slots[:, step, :, None, :] & same[:, None, :, None]).reshape(peers * capacity, peers * row_count)
        rows = everyone[:, step, :, :width].reshape(peers * row_count, width)
        arrived.append(
            jnp.dot(chosen.astype(jnp.bfloat16), rows, preferred_element_type=jnp.float32).astype(jnp.bfloat16)
        )
    arrived = jnp.stack(arrived)
    gathered = lax.all_gather(arrived, "engine", axis=1, tiled=True)

    top = jnp.max(jnp.abs(held_in), axis=(0, 2)).astype(jnp.float32)
    scale_in = (top + EPSILON) / quant_levels
    quant_in = jnp.floor(held_in.astype(jnp.float32) / scale_in[None, :, None, :] + 0.5).astype(jnp.bfloat16)
    quant_in = jnp.transpose(quant_in, (1, 0, 2, 3)).reshape(2, width, units)
    all_in_scales = lax.all_gather(scale_in, "ep", axis=0, tiled=False)
    in_scales = lax.dynamic_index_in_dim(all_in_scales, mine, 0, keepdims=True)
    projected = jnp.einsum("snd,mdf->msnf", gathered, quant_in, preferred_element_type=jnp.float32)
    projected = projected * scale_in[:, None, None, :]
    hidden = (jax.nn.silu(projected[0]) * projected[1]).astype(jnp.bfloat16)
    hidden = lax.all_gather(hidden, "engine", axis=0, tiled=False)
    hidden = jnp.concatenate([hidden[e] for e in range(engines)], axis=-1)
    columns = held_down.reshape(-1, hidden_units)
    summed = jnp.einsum("snf,cf->nsc", hidden, columns, preferred_element_type=jnp.float32)
    outcome = (summed * scale_out.reshape(-1)).astype(jnp.bfloat16)
    outcome = outcome.reshape(engines * peers, capacity, steps, -1)
    returned = lax.all_to_all(outcome, BOTH, split_axis=0, concat_axis=0, tiled=True)
    returned = returned.reshape(engines, peers * capacity, steps, -1)

    wanted = route_ids[..., None] == numbers
    weights = jnp.sum(jnp.where(wanted, route_weights[..., None], 0.0), axis=2)
    filled = first_slots(jnp.any(wanted, axis=2), capacity)
    mixing = jnp.where(filled, weights[:, None], 0.0)
    mixing = jnp.transpose(mixing, (0, 2, 3, 1)).reshape(steps, row_count, peers * capacity)
    combined = jnp.stack(
        [
            jnp.einsum(
                "il,eld->ied", mixing[step], returned[:, :, step].astype(jnp.float32), precision=lax.Precision.HIGHEST
            )
            for step in range(steps)
        ]
    )
    combined = combined.reshape(steps, row_count, width)
    return (combined.astype(jnp.bfloat16), in_scales, out_scales.reshape(1, -1))


def solution(mesh):
    placed = (
        P(None, ("engine", "ep"), None),
        P(None, ("engine", "ep"), None),
        P(None, ("engine", "ep"), None),
        P(),
        P(None, None, ("engine", "ep"), None),
        P(None, None, ("engine", "ep")),
    )
    return jax.shard_map(
        shards,
        mesh=mesh,
        in_specs=placed,
        out_specs=(P(None, ("engine", "ep"), None), P("ep", None, "engine"), P("ep", "engine")),
        check_vma=False,
    )
```

time: 536 us -> 456 us (0.85)
  waiting for transfers between devices: 349 us -> 186 us
  blocking collectives: 0 us -> 134 us
  local copies, waits for them, and re-layouts: 69.4 us -> 35.1 us
  starting transfers between devices: 51.1 us -> 29.7 us
  other arithmetic: 22.6 us -> 29.3 us
    all_to_all x7 -> x3, waiting for transfers between devices: 340 us -> 29.8 us  [the longest x1 29.8 us: shards(): lax.all_to_all(parts, BOTH, split_axis=0, concat_axis=0, tiled=True)]
    all_gather x4 -> x3, waiting for transfers between devices: 9.71 us -> 156 us  [the longest x1 115 us: shards(): everyone = lax.all_gather(payload, 'ep', axis=0, tiled=False)]
    all_gather x0 -> x2, blocking collectives: none -> 134 us  [the longest x1 83.1 us: shards(): all_in_scales = lax.all_gather(scale_in, 'ep', axis=0, tiled=False)]
    all_to_all x5 -> x0, local copies, waits for them, and re-layouts: 32.9 us -> none  [the longest x2 22.3 us: shards(): lax.all_to_all(sorted_in, 'ep', split_axis=0, concat_axis=2, tiled=True)]
    all_to_all x7 -> x3, starting transfers between devices: 50.5 us -> 29.4 us  [the longest x1 16.5 us: shards(): lax.all_to_all(parts, BOTH, split_axis=0, concat_axis=0, tiled=True)]
    gather x2 -> x0, local copies, waits for them, and re-layouts: 8.82 us -> none  [the longest x1 6.39 us: shards(): sorted_in = jnp.take(expert_in, owners, axis=0)]
    floor x1 -> x0, local copies, waits for them, and re-layouts: 8.67 us -> none  [shards(): jnp.floor(held_in.astype(jnp.float32) / scale_in[:, :, None, :] + 0.5)]
    dot_general x0 -> x2, local copies, waits for them, and re-layouts: none -> 8.39 us  [shards(): jnp.einsum('il,eld->ied', mixing[step], returned[:, :, step].astype(jnp.f...]
  transfers between devices with their start and end apart: 11 -> 6, of which waited for: 8 -> 3; matrix products, arithmetic and copies ran while one was open for 20% -> 13% of each run, Pallas kernels for 0% -> 0%
where the time goes in v1:
time: 456 us; the launch traced here: 455 us
  waiting for transfers between devices  186 us (41%)
  blocking collectives  134 us (29%)
  local copies, waits for them, and re-layouts  35.1 us (8%)
  starting transfers between devices  29.7 us (7%)
  other arithmetic  29.3 us (6%)
  matrix products  25.3 us (6%)
  between operations  16 us (4%)
    all_gather x1, waiting for transfers between devices, shards(): everyone = lax.all_gather(payload, 'ep', axis=0, tiled=False)  115 us
    all_gather x1, blocking collectives, shards(): all_in_scales = lax.all_gather(scale_in, 'ep', axis=0, tiled=False)  83.1 us
    all_gather x1, blocking collectives, shards(): all_down_scales = lax.all_gather(down_scale, 'ep', axis=1, tiled=True)  50.6 us
    all_gather x1, waiting for transfers between devices, shards(): gathered = lax.all_gather(arrived, 'engine', axis=1, tiled=True)  41.2 us
    all_to_all x1, waiting for transfers between devices, shards(): lax.all_to_all(parts, BOTH, split_axis=0, concat_axis=0, tiled=True)  29.8 us
    all_to_all x1, starting transfers between devices, shards(): lax.all_to_all(parts, BOTH, split_axis=0, concat_axis=0, tiled=True)  16.5 us
    dot_general x1, matrix products, shards(): jnp.einsum('snd,mdf->msnf', gathered, quant_in, preferred_element_type=jn...  11.1 us
  transfers between devices with their start and end apart: 6, of which 3 were waited for; matrix products, arithmetic and copies ran while one was open for 13% of the time, Pallas kernels for 0%

profile of v1, /device:TPU:1, one launch (start us, length us, event | category | flops | bytes accessed | tf_op | source)
XLA Modules:
  0.0 455.3 jit_solution(4682727593949899629)
XLA Ops:
  7.9 1.6 fusion.22
  9.5 3.6 fusion.27
  13.1 3.5 pad_maximum_fusion
  16.6 16.5 %all-to-all-start.1 = ((bf16[256,2,16,384]{3,2,1,0:T(8,128)(2,1)}), bf16[256,2,16,384]{3,2,1,0:T(8,128)(2,1)}, u32[]{:S(2)}, u32[]{:S(2)}) async-start(bf16[256,2,16,384]{3,2,1,0:T(8,128)(2,1)} %pad_maximum_fusion), calls=%async_computation.1 | async-start | bytes 12582912 | tf_op jit(solution)/shard_map/all_to_all | solution.py:35
  33.2 115.3 %all-gather.11.cloned.1.call-done = bf16[128,8,4224]{2,1,0:T(8,128)(2,1)} async-done(((bf16[2,8,4224]{2,1,0:T(8,128)(2,1)}), bf16[128,8,4224]{2,1,0:T(8,128)(2,1)}) %all-gather.11.cloned.1.call-update) | async-done | bytes 8650768 | tf_op jit(solution)/shard_map/all_gather | solution.py:32
  148.4 3.2 compare_reduce_fusion
  152.1 1.4 broadcast_and_fusion.1
  153.5 2.6 and.103
  156.1 2.6 and.107
  158.7 2.9 fusion.2
  161.7 2.9 fusion.3
  164.6 1.6 pad_maximum_fusion.1
  168.0 2.4 fusion.6
  170.5 29.8 %all-to-all-done.1 = bf16[256,2,16,384]{3,2,1,0:T(8,128)(2,1)} async-done(((bf16[256,2,16,384]{3,2,1,0:T(8,128)(2,1)}), bf16[256,2,16,384]{3,2,1,0:T(8,128)(2,1)}, u32[]{:S(2)}, u32[]{:S(2)}) %all-to-all-start.1) | async-done | bytes 6291488 | tf_op jit(solution)/shard_map/all_to_all | solution.py:35
  200.2 5.0 %all-to-all-start = ((bf16[64,16,1536]{2,1,0:T(8,128)(2,1)}), bf16[64,16,1536]{2,1,0:T(8,128)(2,1)S(1)}, u32[]{:S(2)}, u32[]{:S(2)}) async-start(bf16[64,16,1536]{2,1,0:T(8,128)(2,1)} %fusion.6), calls=%async_computation | async-start | bytes 6291456 | tf_op jit(solution)/shard_map/all_to_all | solution.py:42
  205.5 3.6 abs_reduce_fusion
  209.1 7.6 %floor_convert_fusion = bf16[256,2,16,384]{3,2,0,1:T(8,128)(2,1)} fusion(bf16[256,2,16,384]{3,2,1,0:T(8,128)(2,1)} %all-to-all-done.1, f32[2,384]{1,0:T(2,128)S(1)} %get-tuple-element.41), kind=kLoop, calls=%fused_computation | loop fusion | flops 15728640 | bytes 12585984 | tf_op jit(solution)/shard_map/convert_element_type | solution.py:61
  216.7 41.2 %all-gather.7.cloned.1.call-done = bf16[2,512,4096]{2,1,0:T(8,128)(2,1)} async-done(((bf16[2,128,4096]{2,1,0:T(8,128)(2,1)}), bf16[2,512,4096]{2,1,0:T(8,128)(2,1)}) %all-gather.7.cloned.1.call-update) | async-done | bytes 8388624 | tf_op jit(solution)/shard_map/all_gather | solution.py:57
  257.8 11.1 %multiply_bitcast_fusion = f32[2,2,512,384]{2,3,1,0:T(8,128)S(1)} fusion(bf16[2,4096,384,1]{2,1,3,0:T(8,128)(2,1)} %bitcast.114, bf16[2,512,4096]{2,1,0:T(8,128)(2,1)} %all-gather.7.cloned.1.call-done, f32[2,384]{1,0:T(2,128)S(1)} %get-tuple-element.41), kind=kOutput, calls=%fused_computation.26 | convolution fusion | flops 6443237376 | bytes 17828864 | tf_op jit(solution)/shard_map/snd,mdf->msnf/dot_general | solution.py:65
  268.9 1.4 fusion.20
  270.3 2.3 copy.115
  275.2 50.6 %all_gather.24 = f32[64,1024]{0,1:T(8,128)S(1)} all-gather(f32[64,16]{0,1:T(8,128)S(1)} %add_multiply_fusion), channel_id=1, replica_groups=mesh['engine'=4,'ep'=64] {'ep'}, dimensions={1}, use_global_device_ids=true | all-gather | bytes 266240 | tf_op jit(solution)/shard_map/all_gather | solution.py:41
  325.8 1.1 constant_dynamic-slice_fusion
  327.0 3.7 slice_bitcast_fusion.7
  330.7 5.3 %fusion.15 = bf16[512,2,1024]{2,0,1:T(8,128)(2,1)S(1)} fusion(f32[1024]{0:T(1024)S(1)} %get-tuple-element.29, bf16[1024,1536,1]{1,0,2:T(8,128)(2,1)S(1)} %bitcast.117, bf16[2,512,384]{2,1,0:T(8,128)(2,1)} %get-tuple-element.23, bf16[2,512,384]{2,1,0:T(8,128)(2,1)} %get-tuple-element.24, bf16[2,512,384]{2,1,0:T(8,128)(2,1)} %get-tuple-element.25, ...), kind=kOutput, calls=%fused_computation.28 | convolution fusion | flops 3235905536 | bytes 8392704 | tf_op jit(solution)/shard_map/snf,cf->nsc/dot_general | solution.py:71
  335.9 3.5 copy.124
  339.4 7.9 %all-to-all-start.2 = ((bf16[256,2,2,1024]{3,2,1,0:T(2,128)(2,1)}), bf16[256,2,2,1024]{3,2,1,0:T(2,128)(2,1)S(1)}, u32[]{:S(2)}, u32[]{:S(2)}) async-start(bf16[256,2,2,1024]{3,2,1,0:T(2,128)(2,1)} %bitcast.113), calls=%async_computation.2 | async-start | bytes 4194304 | tf_op jit(solution)/shard_map/all_to_all | solution.py:74
  348.7 83.1 %all-gather.2 = f32[64,2,384]{2,1,0:T(2,128)S(1)} all-gather(f32[1,2,384]{2,1,0:T(2,128)S(1)} %get-tuple-element.40), channel_id=3, replica_groups=mesh['engine'=4,'ep'=64] {'ep'}, dimensions={0}, use_global_device_ids=true | all-gather | bytes 199680 | tf_op jit(solution)/shard_map/all_gather | solution.py:63
  432.3 4.2 fusion.28
  436.5 4.8 %copy.127 = bf16[4,128,1,1024]{1,3,0,2:T(8,128)(2,1)S(1)} copy(bf16[4,128,1,1024]{3,2,1,0:T(2,128)(2,1)} %get-tuple-element.26) | data formatting | bytes 2097152 | tf_op jit(solution)/shard_map/il,eld->ied/dot_general | solution.py:84
  441.3 3.6 copy.128
  445.9 2.2 fusion.5
  (50 shorter events, 7.5 us)
Async XLA Ops:
  7.2 141.3 %all-gather.11.cloned.1.call-start = ((), (), s32[]{:S(2)}) async-start(), calls=%async_computation.5 | async-start | bytes 8785920 | tf_op jit(solution)/shard_map/all_gather | solution.py:32
  16.6 183.7 %all-to-all-start.1 = ((bf16[256,2,16,384]{3,2,1,0:T(8,128)(2,1)}), bf16[256,2,16,384]{3,2,1,0:T(8,128)(2,1)}, u32[]{:S(2)}, u32[]{:S(2)}) async-start(bf16[256,2,16,384]{3,2,1,0:T(8,128)(2,1)} %pad_maximum_fusion), calls=%async_computation.1 | async-start | bytes 12582912 | tf_op jit(solution)/shard_map/all_to_all | solution.py:35
  33.1 224.7 %all-gather.7.cloned.1.call-start = ((), (), s32[]{:S(2)}) async-start(), calls=%async_computation.3 | async-start | bytes 10485760 | tf_op jit(solution)/shard_map/all_gather | solution.py:57
  164.6 2.6 copy-start
  200.2 130.4 %all-to-all-start = ((bf16[64,16,1536]{2,1,0:T(8,128)(2,1)}), bf16[64,16,1536]{2,1,0:T(8,128)(2,1)S(1)}, u32[]{:S(2)}, u32[]{:S(2)}) async-start(bf16[64,16,1536]{2,1,0:T(8,128)(2,1)} %fusion.6), calls=%async_computation | async-start | bytes 6291456 | tf_op jit(solution)/shard_map/all_to_all | solution.py:42
  205.2 121.7 %all-gather.9.cloned.1.call-start = ((), (), s32[]{:S(2)}) async-start(), calls=%async_computation.4 | async-start | bytes 3932160 | tf_op jit(solution)/shard_map/all_gather | solution.py:68
  268.9 3.7 copy-start.5
  339.4 7.9 %copy-start.3 = (s32[2,8,8]{2,1,0:T(8,128)S(1)}, s32[2,8,8]{2,1,0:T(8,128)}, u32[]{:S(2)}) copy-start(s32[2,8,8]{2,1,0:T(8,128)} %param.7) | copy-start | bytes 1540
  339.4 8.1 %copy-start.4 = (f32[2,8,8]{2,1,0:T(8,128)S(1)}, f32[2,8,8]{2,1,0:T(8,128)}, u32[]{:S(2)}) copy-start(f32[2,8,8]{2,1,0:T(8,128)} %param.8) | copy-start | bytes 1540
  339.4 8.5 %copy-start.2 = (f32[1,1024]{0,1:T(8,128)S(1)}, f32[1,1024]{0,1:T(8,128)}, u32[]{:S(2)}) copy-start(f32[1,1024]{0,1:T(8,128)} %get-tuple-element.28) | copy-start | bytes 12292
  339.4 92.9 %all-to-all-start.2 = ((bf16[256,2,2,1024]{3,2,1,0:T(2,128)(2,1)}), bf16[256,2,2,1024]{3,2,1,0:T(2,128)(2,1)S(1)}, u32[]{:S(2)}, u32[]{:S(2)}) async-start(bf16[256,2,2,1024]{3,2,1,0:T(2,128)(2,1)} %bitcast.113), calls=%async_computation.2 | async-start | bytes 4194304 | tf_op jit(solution)/shard_map/all_to_all | solution.py:74
  436.5 4.8 %copy-start.1 = (bf16[4,128,1,1024]{3,2,1,0:T(2,128)(2,1)S(1)}, bf16[4,128,1,1024]{3,2,1,0:T(2,128)(2,1)}, u32[]{:S(2)}) copy-start(bf16[4,128,1,1024]{3,2,1,0:T(2,128)(2,1)} %get-tuple-element.27) | copy-start | bytes 3145732
Sparse Core Ops, SparseCore 0:
  10.7 137.7 all-gather.10
  166.3 91.4 all-gather.6
  272.7 39.9 all-gather.8

commit v2 on v1

v2 whole, which is shorter than its diff:
```python
import jax
import jax.numpy as jnp
from jax import lax
from jax.experimental import pallas as pl
from jax.experimental.pallas import tpu as pltpu
from jax.sharding import PartitionSpec as P


EPSILON = 1e-06
quant_levels = 31.0
BOTH = ("engine", "ep")
MESH = pl.DeviceIdType.MESH
XS, ZS, CS, YS = 4, 8, 2, 4


def place():
    p = lax.axis_index("ep")
    return lax.axis_index("engine"), p // (ZS * CS), (p // CS) % ZS, p % CS


def device(y, x, z, c):
    return {"engine": y, "ep": x * (ZS * CS) + z * CS + c}


def peers_of(kind):
    y, x, z, c = place()
    if kind == "z":
        return [device(y, x, (z + d) % ZS, c) for d in (4, 3, 5, 2, 6, 1, 7)]
    if kind == "x":
        return [device(y, (x + d) % XS, z, c) for d in (2, 1, 3)]
    if kind == "y":
        return [device((y + d) % YS, x, z, c) for d in (2, 1, 3)]
    if kind == "c":
        return [device(y, x, z, 1 - c)]
    return [device(y, (x + d) % XS, z, (c + f) % CS) for f in (0, 1) for d in range(XS) if (d, f) != (0, 0)]


def greet(kinds):
    barrier = pltpu.get_barrier_semaphore()
    count = 0
    for kind in kinds:
        for peer in peers_of(kind):
            pl.semaphore_signal(barrier, inc=1, device_id=peer, device_id_type=MESH)
            count += 1
    pl.semaphore_wait(barrier, count)


def send(src, dst, send_sem, recv_sem, peer):
    copy = pltpu.make_async_remote_copy(
        src_ref=src, dst_ref=dst, send_sem=send_sem, recv_sem=recv_sem, device_id=peer, device_id_type=MESH
    )
    copy.start()
    return copy


def await_bytes(like, sem):
    pltpu.make_async_copy(like, like, sem).wait()


def dispatch_kernel(tok_ref, meta_ref, all_tok, plane, cols, sent, got, own):
    y, x, z, c = place()
    greet(("z", "x", "y", "c"))
    mine = pltpu.make_async_copy(tok_ref, all_tok.at[c, x, z], own)
    mine.start()
    for peer in peers_of("z"):
        send(tok_ref, all_tok.at[c, x, z], sent.at[0], got.at[0], peer)
        send(meta_ref, plane.at[c, x, z], sent.at[1], got.at[1], peer)
    plane[c, x, z] = meta_ref[...]
    mine.wait()
    await_bytes(plane.at[c, x, pl.ds(0, ZS - 1)], got.at[1])
    await_bytes(all_tok.at[c, x, pl.ds(0, ZS - 1)], got.at[0])
    for peer in peers_of("x"):
        send(all_tok.at[c, x], all_tok.at[c, x], sent.at[2], got.at[2], peer)
        send(plane.at[c, x], plane.at[c, x], sent.at[3], got.at[3], peer)
    for peer in peers_of("y"):
        send(plane.at[c, x], cols.at[y], sent.at[4], got.at[4], peer)
    cols[y] = plane[c, x]
    await_bytes(plane.at[c, pl.ds(0, XS - 1)], got.at[3])
    await_bytes(all_tok.at[c, pl.ds(0, XS - 1)], got.at[2])
    for peer in peers_of("c"):
        send(all_tok.at[c], all_tok.at[c], sent.at[5], got.at[5], peer)
        send(plane.at[c], plane.at[c], sent.at[6], got.at[6], peer)
    await_bytes(cols.at[pl.ds(0, YS - 1)], got.at[4])
    await_bytes(plane.at[c], got.at[6])
    await_bytes(all_tok.at[c], got.at[5])
    await_bytes(all_tok.at[c, x, pl.ds(0, ZS - 1)], sent.at[0])
    await_bytes(plane.at[c, x, pl.ds(0, ZS - 1)], sent.at[1])
    await_bytes(all_tok.at[c, pl.ds(0, XS - 1)], sent.at[2])
    await_bytes(plane.at[c, pl.ds(0, XS - 1)], sent.at[3])
    await_bytes(cols.at[pl.ds(0, YS - 1)], sent.at[4])
    await_bytes(all_tok.at[c], sent.at[5])
    await_bytes(plane.at[c], sent.at[6])


def dispatch(tok, meta):
    rows, width = tok.shape
    vmem = pl.BlockSpec(memory_space=pltpu.VMEM)
    return pl.pallas_call(
        dispatch_kernel,
        out_shape=(
            jax.ShapeDtypeStruct((CS, XS, ZS, rows, width), tok.dtype),
            jax.ShapeDtypeStruct((CS, XS, ZS) + meta.shape, meta.dtype),
            jax.ShapeDtypeStruct((YS, ZS) + meta.shape, meta.dtype),
        ),
        in_specs=[vmem, vmem],
        out_specs=(pl.BlockSpec(memory_space=pl.ANY), vmem, vmem),
        scratch_shapes=[pltpu.SemaphoreType.DMA((7,)), pltpu.SemaphoreType.DMA((7,)), pltpu.SemaphoreType.DMA],
        compiler_params=pltpu.CompilerParams(collective_id=0, has_side_effects=True),
        cost_estimate=pl.CostEstimate(flops=20_000_000_000, bytes_accessed=10_000_000, transcendentals=0),
        name="dispatch",
    )(tok, meta)


def return_kernel(outcome, mixing, out, first, partial, second, total, third, sent, got, own):
    steps = outcome.shape[0]
    y, x, z, c = place()
    here = c * XS + x
    greet(("xc", "z", "y"))
    locals_ = []
    for s in range(steps):
        local = pltpu.make_async_copy(outcome.at[s, :, here], first.at[s, here], own.at[s])
        local.start()
        locals_.append(local)
        for f, d in ((0, 2), (0, 1), (0, 3), (1, 2), (1, 1), (1, 3), (1, 0)):
            there_x, there_c = (x + d) % XS, (c + f) % CS
            src = outcome.at[s, :, there_c * XS + there_x]
            send(src, first.at[s, here], sent.at[s], got.at[s], device(y, there_x, z, there_c))
    for s in range(steps):
        locals_[s].wait()
        await_bytes(first.at[s, pl.ds(0, XS * CS - 1)], got.at[s])
        rows = first[s].reshape(-1, first.shape[-1]).astype(jnp.float32)
        sums = jnp.dot(mixing[s], rows, precision=lax.Precision.HIGHEST, preferred_element_type=jnp.float32)
        partial[s] = sums.astype(partial.dtype).reshape(partial.shape[1:])
        second[s, z] = partial[s, z]
        for d in (4, 3, 5, 2, 6, 1, 7):
            there = (z + d) % ZS
            send(partial.at[s, there], second.at[s, z], sent.at[steps + s], got.at[steps + s], device(y, x, there, c))
    sums = []
    for s in range(steps):
        await_bytes(second.at[s, pl.ds(0, ZS - 1)], got.at[steps + s])
        sums.append(jnp.sum(second[s].astype(jnp.float32), axis=0).reshape(YS, -1, second.shape[-1]))
    total[...] = jnp.concatenate(sums, axis=1).astype(total.dtype)
    third[y] = total[y]
    for d in (2, 1, 3):
        there = (y + d) % YS
        send(total.at[there], third.at[y], sent.at[2 * steps], got.at[2 * steps], device(there, x, z, c))
    await_bytes(third.at[pl.ds(0, YS - 1)], got.at[2 * steps])
    columns = third.shape[-1]
    for e in range(YS):
        out[:, e * columns : (e + 1) * columns] = third[e]
    for s in range(steps):
        await_bytes(first.at[s, pl.ds(0, XS * CS - 1)], sent.at[s])
        await_bytes(second.at[s, pl.ds(0, ZS - 1)], sent.at[steps + s])
    await_bytes(third.at[pl.ds(0, YS - 1)], sent.at[2 * steps])


def give_back(outcome, mixing, row_count):
    steps, _, _, block, columns = outcome.shape
    vmem = pl.BlockSpec(memory_space=pltpu.VMEM)
    kept = outcome.dtype
    return pl.pallas_call(
        return_kernel,
        out_shape=jax.ShapeDtypeStruct((steps * row_count, YS * columns), kept),
        in_specs=[pl.BlockSpec(memory_space=pl.ANY), vmem],
        out_specs=vmem,
        scratch_shapes=[
            pltpu.VMEM((steps, CS * XS, YS, block, columns), kept),
            pltpu.VMEM((steps, ZS, YS * row_count, columns), kept),
            pltpu.VMEM((steps, ZS, YS * row_count, columns), kept),
            pltpu.VMEM((YS, steps * row_count, columns), kept),
            pltpu.VMEM((YS, steps * row_count, columns), kept),
            pltpu.SemaphoreType.DMA((2 * steps + 1,)),
            pltpu.SemaphoreType.DMA((2 * steps + 1,)),
            pltpu.SemaphoreType.DMA((steps,)),
        ],
        compiler_params=pltpu.CompilerParams(
            collective_id=1, has_side_effects=True, vmem_limit_bytes=48 * 1024 * 1024
        ),
        cost_estimate=pl.CostEstimate(flops=20_000_000_000, bytes_accessed=10_000_000, transcendentals=0),
        name="give_back",
    )(outcome, mixing)


def first_slots(named, capacity, axis):
    counted = named.astype(jnp.int32)
    before = jnp.cumsum(counted, axis=axis) - counted
    return jnp.stack([named & (before == slot) for slot in range(capacity)])


def layer(tokens, route_ids, route_weights, placement, expert_in, expert_down):
    experts = placement.shape[0]
    engines = lax.axis_size("engine")
    peers = lax.axis_size("ep")
    me = lax.axis_index("ep")
    _, _, my_z, _ = place()
    steps, row_count, width = tokens.shape
    capacity = 2
    tops = route_ids.shape[2]
    hidden_units = expert_in.shape[3]
    units = hidden_units // engines
    columns = width // engines
    numbers = jnp.arange(experts, dtype=jnp.int32)

    meta = jnp.concatenate([route_ids.astype(jnp.float32), route_weights], axis=2).reshape(steps * row_count, -1)
    meta = jnp.pad(meta, ((0, 0), (0, 128 - 2 * tops)))
    parts = jnp.concatenate([expert_in[..., e * units : (e + 1) * units] for e in range(engines)], axis=0)
    held_in = lax.all_to_all(parts, BOTH, split_axis=0, concat_axis=0, tiled=True)
    everyone, plane, cols = dispatch(tokens.reshape(steps * row_count, width), meta)

    named = jnp.any(plane[..., :tops] == me.astype(jnp.float32), axis=-1)
    named = named.reshape(peers, steps, row_count)
    slots = first_slots(named, capacity, 2)
    blocks = jnp.eye(peers, dtype=jnp.bool_)
    turns = jnp.eye(steps, dtype=jnp.bool_)
    slots = jnp.transpose(slots, (2, 1, 0, 3))
    chosen = slots[:, :, :, None, None, :] & blocks[None, :, None, :, None, None] & turns[:, None, None, None, :, None]
    chosen = chosen.reshape(steps * peers * capacity, peers * steps * row_count).astype(jnp.bfloat16)
    arrived = jnp.dot(chosen, everyone.reshape(-1, width), preferred_element_type=jnp.float32).astype(jnp.bfloat16)
    arrived = arrived.reshape(steps, peers * capacity, width)
    gathered = lax.all_gather(arrived, "engine", axis=1, tiled=True)

    near = jnp.arange(CS * XS, dtype=jnp.int32)
    near = (near % XS) * (ZS * CS) + my_z * CS + near // XS
    ids = cols[..., :tops].reshape(YS, ZS, steps, row_count, tops)
    wanted = ids[..., None] == near.astype(jnp.float32)
    strength = cols[..., tops : 2 * tops].reshape(YS, ZS, steps, row_count, tops)
    strength = jnp.sum(jnp.where(wanted, strength[..., None], 0.0), axis=4)
    filled = first_slots(jnp.any(wanted, axis=4), capacity, 3)
    shares = jnp.transpose(jnp.where(filled, strength[None], 0.0), (3, 2, 1, 4, 5, 0))
    same_y, same_z = jnp.eye(YS, dtype=jnp.bool_), jnp.eye(ZS, dtype=jnp.bool_)
    same = same_y[None, None, :, None, None, :, None, None] & same_z[None, :, None, None, None, None, :, None]
    mixing = jnp.where(same, shares[:, :, :, :, :, None, None, :], 0.0)
    mixing = mixing.reshape(steps, ZS * YS * row_count, CS * XS * YS * ZS * capacity)

    down = jnp.transpose(expert_down, (0, 2, 1))
    down_top = jnp.max(jnp.abs(down), axis=2).astype(jnp.float32)
    down_scale = (down_top + EPSILON) / quant_levels
    quant_down = jnp.floor(down.astype(jnp.float32) / down_scale[:, :, None] + 0.5).astype(jnp.bfloat16)
    held_down = lax.all_to_all(quant_down, "ep", split_axis=0, concat_axis=0, tiled=True)
    owners = jnp.sum(jnp.where(placement[None, :] == numbers[:, None], numbers[None, :], 0), axis=1)
    both_orders = jnp.stack([down_scale[owners], down_scale], axis=1)
    own_columns = (jnp.arange(peers) == me)[None, None, :, None]
    spread = jnp.where(own_columns, both_orders[:, :, None, :], 0.0).reshape(experts, 2, columns)
    both_scales = lax.psum_scatter(spread, "ep", scatter_dimension=0, tiled=True)
    out_scales, scale_out = both_scales[:, 0], both_scales[0, 1]

    top = jnp.max(jnp.abs(held_in), axis=(0, 2)).astype(jnp.float32)
    scale_in = (top + EPSILON) / quant_levels
    quant_in = jnp.floor(held_in.astype(jnp.float32) / scale_in[None, :, None, :] + 0.5).astype(jnp.bfloat16)
    quant_in = jnp.transpose(quant_in, (1, 0, 2, 3)).reshape(2, width, units)
    my_slot = jnp.sum(jnp.where(numbers == me, placement, 0))
    spread_in = jnp.where((numbers == my_slot)[:, None, None], scale_in[None], 0.0)
    projected = jnp.einsum("snd,mdf->msnf", gathered, quant_in, preferred_element_type=jnp.float32)
    projected = projected * scale_in[:, None, None, :]
    hidden = (jax.nn.silu(projected[0]) * projected[1]).astype(jnp.bfloat16)
    hidden = lax.all_gather(hidden, "engine", axis=0, tiled=False)
    spread_in, hidden, scale_out = lax.optimization_barrier((spread_in, hidden, scale_out))
    in_scales = lax.psum_scatter(spread_in, "ep", scatter_dimension=0, tiled=True)
    hidden = jnp.concatenate([hidden[e] for e in range(engines)], axis=-1)
    summed = jnp.einsum(
        "snf,cf->snc", hidden, held_down.reshape(-1, hidden_units), preferred_element_type=jnp.float32
    )
    outcome = (summed * scale_out).astype(jnp.bfloat16)
    outcome = outcome.reshape(steps, YS, CS * XS, ZS * capacity, columns)
    combined = give_back(outcome, mixing, row_count)
    return (combined.reshape(steps, row_count, width), in_scales, out_scales)


def solution(mesh):
    placed = (
        P(None, ("engine", "ep"), None),
        P(None, ("engine", "ep"), None),
        P(None, ("engine", "ep"), None),
        P(),
        P(None, None, ("engine", "ep"), None),
        P(None, None, ("engine", "ep")),
    )
    return jax.shard_map(
        layer,
        mesh=mesh,
        in_specs=placed,
        out_specs=(P(None, ("engine", "ep"), None), P("ep", None, "engine"), P("ep", "engine")),
        check_vma=False,
    )
```

time: 456 us -> 583 us (1.28)
  Pallas kernels: 0 us -> 143 us
  blocking collectives: 134 us -> 0 us
  waiting for transfers between devices: 186 us -> 266 us
  local copies, waits for them, and re-layouts: 35.1 us -> 74.2 us
  starting transfers between devices: 29.7 us -> 14.6 us
  other arithmetic: 29.3 us -> 43.3 us
    all_gather x3 -> x2, waiting for transfers between devices: 156 us -> 0.01 us  [the longest x1 0.01 us: layer(): gathered = lax.all_gather(arrived, 'engine', axis=1, tiled=True)]
    pallas_call x0 -> x2, Pallas kernels: none -> 143 us  [the longest x1 95.3 us: dispatch(): pl.pallas_call(dispatch_kernel, out_shape=(jax.ShapeDtypeStruct((CS, XS,...]
    all_gather x2 -> x0, blocking collectives: 134 us -> none  [the longest x1 83.1 us: shards(): all_in_scales = lax.all_gather(scale_in, 'ep', axis=0, tiled=False)]
    unnamed x3 -> x6, waiting for transfers between devices: 0.05 us -> 125 us
    all_to_all x3 -> x2, waiting for transfers between devices: 29.8 us -> 141 us  [the longest x1 139 us: layer(): lax.all_to_all(parts, BOTH, split_axis=0, concat_axis=0, tiled=True)]
    broadcast_in_dim x0 -> x9, local copies, waits for them, and re-layouts: none -> 36 us  [the longest x6 35.7 us: layer(): mixing = jnp.where(same, shares[:, :, :, :, :, None, None, :], 0.0)]
    all_to_all x3 -> x2, starting transfers between devices: 29.4 us -> 14.5 us  [the longest x1 9.15 us: layer(): lax.all_to_all(parts, BOTH, split_axis=0, concat_axis=0, tiled=True)]
    and x5 -> x1, local copies, waits for them, and re-layouts: 5.5 us -> 20.4 us  [layer(): slots[:, :, :, None, None, :] & blocks[None, :, None, :, None, None]]
  transfers between devices with their start and end apart: 6 -> 6, of which waited for: 3 -> 3; matrix products, arithmetic and copies ran while one was open for 13% -> 16% of each run, Pallas kernels for 0% -> 8%
where the time goes in v2:
time: 583 us; the launch traced here: 581 us
  waiting for transfers between devices  266 us (46%)
  Pallas kernels  143 us (25%)
  local copies, waits for them, and re-layouts  74.2 us (13%)
  other arithmetic  43.3 us (7%)
  matrix products  23.7 us (4%)
  between operations  15.9 us (3%)
  starting transfers between devices  14.6 us (3%)
    all_to_all x1, waiting for transfers between devices, layer(): lax.all_to_all(parts, BOTH, split_axis=0, concat_axis=0, tiled=True)  139 us
    unnamed x6, waiting for transfers between devices  125 us
    pallas_call x1, Pallas kernels, dispatch(): pl.pallas_call(dispatch_kernel, out_shape=(jax.ShapeDtypeStruct((CS, XS,...  95.3 us
    pallas_call x1, Pallas kernels, give_back(): pl.pallas_call(return_kernel, out_shape=jax.ShapeDtypeStruct((steps * row...  48.1 us
    broadcast_in_dim x6, local copies, waits for them, and re-layouts, layer(): mixing = jnp.where(same, shares[:, :, :, :, :, None, None, :], 0.0)  35.7 us
    and x1, local copies, waits for them, and re-layouts, layer(): slots[:, :, :, None, None, :] & blocks[None, :, None, :, None, None]  20.4 us
    and x2, other arithmetic, layer(): slots[:, :, :, None, None, :] & blocks[None, :, None, :, None, None]  15.2 us
  transfers between devices with their start and end apart: 6, of which 3 were waited for; matrix products, arithmetic and copies ran while one was open for 16% of the time, Pallas kernels for 8%

profile of v2, /device:TPU:1, one launch (start us, length us, event | category | flops | bytes accessed | tf_op | source)
XLA Modules:
  0.0 581.5 jit_solution(2868341959057201753)
XLA Ops:
  10.2 95.3 %dispatch.1 = (bf16[2,4,8,16,4096]{4,3,2,1,0:T(8,128)(2,1)}, f32[2,4,8,16,128]{4,3,2,1,0:T(8,128)}, f32[4,8,16,128]{3,2,1,0:T(8,128)}) custom-call(bf16[16,4096]{1,0:T(8,128)(2,1)} %bitcast.93, f32[16,128]{1,0:T(8,128)} %pad.4.meta_ref), custom_call_target="tpu_custom_call" | custom-call | flops 20000000000 | bytes 10000000 | tf_op jit(solution)/shard_map/dispatch/pallas_call | solution.py:98
  105.5 2.2 fusion.17
  108.3 1.5 broadcast_and_fusion.1
  109.8 13.7 %broadcast_and_fusion = pred[2,64,2,64,2,8]{5,4,3,2,1,0:T(4,128)(4,1)} fusion(pred[2,2]{1,0:T(4,128)(4,1)S(1)} %iota_compare_fusion.4, pred[2,64,2,64,8]{4,3,2,1,0:T(8,128)(4,1)S(1)} %broadcast_and_fusion.1), kind=kLoop, calls=%fused_computation.1 | loop fusion | flops 262144 | bytes 393220 | tf_op jit(solution)/shard_map/and | solution.py:216
  123.5 20.4 %and.143 = pred[256,1024]{1,0:T(32,128)(4,1)S(1)} reshape(pred[2,64,2,64,2,8]{5,4,3,2,1,0:T(4,128)(4,1)} %broadcast_and_fusion) | data formatting | bytes 524288 | tf_op jit(solution)/shard_map/and | solution.py:216
  144.0 7.0 %convolution_convert_fusion = bf16[256,4096]{1,0:T(8,128)(2,1)} fusion(pred[256,1024]{1,0:T(32,128)(4,1)S(1)} %and.143, bf16[1024,4096]{1,0:T(8,128)(2,1)} %bitcast.94), kind=kOutput, calls=%fused_computation.8 | convolution fusion | flops 2148532224 | bytes 10747904 | tf_op jit(solution)/shard_map/dot_general | solution.py:218
  151.0 3.6 fusion.25
  154.6 3.5 pad_maximum_fusion
  158.0 9.1 %all-to-all-start = ((bf16[256,2,16,384]{3,2,1,0:T(8,128)(2,1)}), bf16[256,2,16,384]{3,2,1,0:T(8,128)(2,1)}, u32[]{:S(2)}, u32[]{:S(2)}) async-start(bf16[256,2,16,384]{3,2,1,0:T(8,128)(2,1)} %pad_maximum_fusion), calls=%async_computation | async-start | bytes 12582912 | tf_op jit(solution)/shard_map/all_to_all | solution.py:207
  169.0 1.2 bitcast_select_fusion
  170.2 2.4 copy.55
  172.6 2.4 fusion.2
  175.0 138.5 %all-to-all-done = bf16[256,2,16,384]{3,2,1,0:T(8,128)(2,1)} async-done(((bf16[256,2,16,384]{3,2,1,0:T(8,128)(2,1)}), bf16[256,2,16,384]{3,2,1,0:T(8,128)(2,1)}, u32[]{:S(2)}, u32[]{:S(2)}) %all-to-all-start) | async-done | bytes 6291488 | tf_op jit(solution)/shard_map/all_to_all | solution.py:207
  313.6 5.3 all-to-all-start.1
  319.0 3.6 abs_reduce_fusion
  322.6 7.5 %floor_convert_fusion = bf16[256,2,16,384]{3,2,0,1:T(8,128)(2,1)} fusion(bf16[256,2,16,384]{3,2,1,0:T(8,128)(2,1)} %all-to-all-done, f32[2,384]{1,0:T(2,128)S(1)} %add_multiply_fusion.1), kind=kLoop, calls=%fused_computation.2 | loop fusion | flops 15728640 | bytes 12585984 | tf_op jit(solution)/shard_map/convert_element_type | solution.py:249
  330.1 11.1 %multiply_bitcast_fusion = f32[2,2,512,384]{2,3,1,0:T(8,128)S(1)} fusion(bf16[2,4096,384,1]{2,1,3,0:T(8,128)(2,1)} %bitcast.89, bf16[2,512,4096]{2,1,0:T(8,128)(2,1)} %all-gather.3.cloned.1.call-done, f32[2,384]{1,0:T(2,128)S(1)} %add_multiply_fusion.1), kind=kOutput, calls=%fused_computation.21 | convolution fusion | flops 6443237376 | bytes 17828864 | tf_op jit(solution)/shard_map/snd,mdf->msnf/dot_general | solution.py:253
  341.7 1.2 copy.52
  343.1 0.8 compare_reduce_fusion
  344.3 1.3 fusion.11
  346.3 6.4 %broadcast_in_dim.157 = f32[2,8,4,8,8,4,8,2]{3,2,1,7,6,5,4,0:T(4,128)} broadcast(f32[2,8,4,8,8,2]{3,2,1,5,4,0:T(4,128)S(1)} %copy.57), dimensions={0,1,2,3,4,7} | broadcast | bytes 1081344 | tf_op jit(solution)/shard_map/jit(_where)/broadcast_in_dim | solution.py:232
  352.7 21.2 %broadcast_in_dim.158 = f32[2,256,512]{1,2,0:T(8,128)S(1)} reshape(f32[2,8,4,8,8,4,8,2]{3,2,1,7,6,5,4,0:T(4,128)} %broadcast_in_dim.157) | data formatting | bytes 2097152 | tf_op jit(solution)/shard_map/jit(_where)/broadcast_in_dim | solution.py:232
  374.4 1.7 broadcast_in_dim.149
  376.1 5.8 broadcast_in_dim.150
  384.2 2.0 dynamic-slice_bitcast_fusion
  386.2 0.8 broadcast_select_fusion.1
  387.0 3.1 slice_bitcast_fusion.3
  390.1 2.7 all-to-all-done.1
  392.9 5.6 multiply_convert_fusion
  398.4 48.1 %give_back.1 = bf16[16,4096]{1,0:T(8,128)(2,1)S(1)} custom-call(bf16[2,4,8,16,1024]{4,3,2,1,0:T(8,128)(2,1)S(1)} %bitcast.88, f32[2,256,512]{2,1,0:T(8,128)S(1)} %broadcast_select_fusion.mixing), custom_call_target="tpu_custom_call" | custom-call | flops 20000000000 | bytes 10000000 | tf_op jit(solution)/shard_map/give_back/pallas_call | solution.py:161
  446.5 125.0 %all-reduce.8.cloned.1.call-done = f32[64,2,384]{2,1,0:T(2,128)} async-done(((f32[64,2,384]{2,1,0:T(2,128)}), f32[64,2,384]{2,1,0:T(2,128)}) %all-reduce.8.cloned.1.call-update) | async-done | bytes 196624
  571.5 1.9 constant_dynamic-slice_fusion.1
  (64 shorter events, 9.7 us)
Async XLA Ops:
  8.0 322.1 %all-gather.3.cloned.1.call-start = ((), (), s32[]{:S(2)}) async-start(), calls=%async_computation.2 | async-start | bytes 10485760 | tf_op jit(solution)/shard_map/all_gather | solution.py:220
  158.0 9.2 %copy-start = (bf16[64,1536,16]{1,2,0:T(8,128)(2,1)S(1)}, bf16[64,1536,16]{1,2,0:T(8,128)(2,1)}, u32[]{:S(2)}) copy-start(bf16[64,1536,16]{1,2,0:T(8,128)(2,1)} %param.11) | copy-start | bytes 9437188
  158.0 155.6 %all-to-all-start = ((bf16[256,2,16,384]{3,2,1,0:T(8,128)(2,1)}), bf16[256,2,16,384]{3,2,1,0:T(8,128)(2,1)}, u32[]{:S(2)}, u32[]{:S(2)}) async-start(bf16[256,2,16,384]{3,2,1,0:T(8,128)(2,1)} %pad_maximum_fusion), calls=%async_computation | async-start | bytes 12582912 | tf_op jit(solution)/shard_map/all_to_all | solution.py:207
  167.2 0.8 copy-start.2
  167.2 217.0 %all-reduce.6.cloned.1.call-start = ((), (), s32[]{:S(2)}) async-start(), calls=%async_computation.4 | async-start | bytes 1048576
  313.6 79.3 %all-to-all-start.1 = ((bf16[64,16,1536]{2,1,0:T(8,128)(2,1)}), bf16[64,16,1536]{2,1,0:T(8,128)(2,1)}, u32[]{:S(2)}, u32[]{:S(2)}) async-start(bf16[64,16,1536]{2,1,0:T(8,128)(2,1)} %fusion.2), calls=%async_computation.1 | async-start | bytes 6291456 | tf_op jit(solution)/shard_map/all_to_all | solution.py:239
  318.9 68.1 %all-gather.5.cloned.1.call-start = ((), (), s32[]{:S(2)}) async-start(), calls=%async_computation.3 | async-start | bytes 3932160 | tf_op jit(solution)/shard_map/all_gather | solution.py:256
  341.2 1.8 copy-start.1
  342.9 228.6 %all-reduce.8.cloned.1.call-start = ((), (), s32[]{:S(2)}) async-start(), calls=%async_computation.5 | async-start | bytes 393216
  373.9 8.2 %copy-start.3 = (u32[256]{0:T(256)S(1)}, u32[256]{0:T(256)}, u32[]{:S(2)}) copy-start(u32[256]{0:T(256)} %constant.104) | copy-start | bytes 3076
Sparse Core Ops, SparseCore 0:
  151.1 142.2 all-gather.2
  343.0 40.1 all-gather.4
Sparse Core Ops, SparseCore 1:
  172.7 202.9 all-reduce.5
  387.1 184.3 all-reduce.7

commit v3 on v2

v3 whole, which is shorter than its diff:
```python
import jax
import jax.numpy as jnp
from jax import lax
from jax.experimental import pallas as pl
from jax.experimental.pallas import tpu as pltpu
from jax.sharding import PartitionSpec as P

EPSILON = 1e-06
quant_levels = 31.0
BOTH = ("engine", "ep")
MESH = pl.DeviceIdType.MESH
XS, ZS, CS, YS = 4, 8, 2, 4


def place():
    p = lax.axis_index("ep")
    return lax.axis_index("engine"), p // (ZS * CS), (p // CS) % ZS, p % CS


def device(y, x, z, c):
    return {"engine": y, "ep": x * (ZS * CS) + z * CS + c}


def peers_of(kind):
    y, x, z, c = place()
    if kind == "z":
        return [device(y, x, (z + d) % ZS, c) for d in (4, 3, 5, 2, 6, 1, 7)]
    if kind == "x":
        return [device(y, (x + d) % XS, z, c) for d in (2, 1, 3)]
    if kind == "y":
        return [device((y + d) % YS, x, z, c) for d in (2, 1, 3)]
    if kind == "c":
        return [device(y, x, z, 1 - c)]
    return [device(y, (x + d) % XS, z, (c + f) % CS) for f in (0, 1) for d in range(XS) if (d, f) != (0, 0)]


def greet(kinds):
    barrier = pltpu.get_barrier_semaphore()
    count = 0
    for kind in kinds:
        for peer in peers_of(kind):
            pl.semaphore_signal(barrier, inc=1, device_id=peer, device_id_type=MESH)
            count += 1
    pl.semaphore_wait(barrier, count)


def send(src, dst, send_sem, recv_sem, peer):
    copy = pltpu.make_async_remote_copy(
        src_ref=src, dst_ref=dst, send_sem=send_sem, recv_sem=recv_sem, device_id=peer, device_id_type=MESH
    )
    copy.start()
    return copy


def await_bytes(like, sem):
    pltpu.make_async_copy(like, like, sem).wait()


def notes_kernel(meta_ref, plane, cols, sent, got):
    y, x, z, c = place()
    greet(("z", "x", "y", "c"))
    for peer in peers_of("z"):
        send(meta_ref, plane.at[c, x, z], sent.at[0], got.at[0], peer)
    plane[c, x, z] = meta_ref[...]
    await_bytes(plane.at[c, x, pl.ds(0, ZS - 1)], got.at[0])
    for peer in peers_of("x"):
        send(plane.at[c, x], plane.at[c, x], sent.at[1], got.at[1], peer)
    for peer in peers_of("y"):
        send(plane.at[c, x], cols.at[y], sent.at[2], got.at[2], peer)
    cols[y] = plane[c, x]
    await_bytes(plane.at[c, pl.ds(0, XS - 1)], got.at[1])
    for peer in peers_of("c"):
        send(plane.at[c], plane.at[c], sent.at[3], got.at[3], peer)
    await_bytes(cols.at[pl.ds(0, YS - 1)], got.at[2])
    await_bytes(plane.at[c], got.at[3])
    await_bytes(plane.at[c, x, pl.ds(0, ZS - 1)], sent.at[0])
    await_bytes(plane.at[c, pl.ds(0, XS - 1)], sent.at[1])
    await_bytes(cols.at[pl.ds(0, YS - 1)], sent.at[2])
    await_bytes(plane.at[c], sent.at[3])


def pass_notes(meta):
    vmem = pl.BlockSpec(memory_space=pltpu.VMEM)
    return pl.pallas_call(
        notes_kernel,
        out_shape=(
            jax.ShapeDtypeStruct((CS, XS, ZS) + meta.shape, meta.dtype),
            jax.ShapeDtypeStruct((YS, ZS) + meta.shape, meta.dtype),
        ),
        in_specs=[vmem],
        out_specs=(vmem, vmem),
        scratch_shapes=[pltpu.SemaphoreType.DMA((4,)), pltpu.SemaphoreType.DMA((4,))],
        compiler_params=pltpu.CompilerParams(collective_id=0, has_side_effects=True),
        name="notes",
    )(meta)


def return_kernel(outcome, mixing, scales, out, heard, first, partial, second, total, third, sent, got, own):
    steps = outcome.shape[0]
    y, x, z, c = place()
    here = c * XS + x
    greet(("xc", "z", "y"))
    locals_ = []
    last = 2 * steps + 1
    heard[here, z] = scales[...]
    for f, d in ((0, 2), (0, 1), (0, 3), (1, 2), (1, 1), (1, 3), (1, 0)):
        peer = device(y, (x + d) % XS, z, (c + f) % CS)
        send(scales, heard.at[here, z], sent.at[last], got.at[last], peer)
    for s in range(steps):
        local = pltpu.make_async_copy(outcome.at[s, :, here], first.at[s, here], own.at[s])
        local.start()
        locals_.append(local)
        for f, d in ((0, 2), (0, 1), (0, 3), (1, 2), (1, 1), (1, 3), (1, 0)):
            there_x, there_c = (x + d) % XS, (c + f) % CS
            src = outcome.at[s, :, there_c * XS + there_x]
            send(src, first.at[s, here], sent.at[s], got.at[s], device(y, there_x, z, there_c))
    for s in range(steps):
        locals_[s].wait()
        await_bytes(first.at[s, pl.ds(0, XS * CS - 1)], got.at[s])
        rows = first[s].reshape(-1, first.shape[-1]).astype(jnp.float32)
        sums = jnp.dot(mixing[s], rows, precision=lax.Precision.HIGHEST, preferred_element_type=jnp.float32)
        partial[s] = sums.astype(partial.dtype).reshape(partial.shape[1:])
        second[s, z] = partial[s, z]
        for d in (4, 3, 5, 2, 6, 1, 7):
            there = (z + d) % ZS
            send(partial.at[s, there], second.at[s, z], sent.at[steps + s], got.at[steps + s], device(y, x, there, c))
    await_bytes(heard.at[pl.ds(0, XS * CS - 1), z], got.at[last])
    for peer in peers_of("z"):
        send(heard.at[:, z], heard.at[:, z], sent.at[last + 1], got.at[last + 1], peer)
    sums = []
    for s in range(steps):
        await_bytes(second.at[s, pl.ds(0, ZS - 1)], got.at[steps + s])
        sums.append(jnp.sum(second[s].astype(jnp.float32), axis=0).reshape(YS, -1, second.shape[-1]))
    total[...] = jnp.concatenate(sums, axis=1).astype(total.dtype)
    third[y] = total[y]
    for d in (2, 1, 3):
        there = (y + d) % YS
        send(total.at[there], third.at[y], sent.at[2 * steps], got.at[2 * steps], device(there, x, z, c))
    await_bytes(third.at[pl.ds(0, YS - 1)], got.at[2 * steps])
    columns = third.shape[-1]
    for e in range(YS):
        out[:, e * columns : (e + 1) * columns] = third[e]
    await_bytes(heard.at[:, pl.ds(0, ZS - 1)], got.at[last + 1])
    await_bytes(heard.at[pl.ds(0, XS * CS - 1), z], sent.at[last])
    await_bytes(heard.at[:, pl.ds(0, ZS - 1)], sent.at[last + 1])
    for s in range(steps):
        await_bytes(first.at[s, pl.ds(0, XS * CS - 1)], sent.at[s])
        await_bytes(second.at[s, pl.ds(0, ZS - 1)], sent.at[steps + s])
    await_bytes(third.at[pl.ds(0, YS - 1)], sent.at[2 * steps])


def give_back(outcome, mixing, scales, row_count):
    steps, _, _, block, columns = outcome.shape
    vmem = pl.BlockSpec(memory_space=pltpu.VMEM)
    kept = outcome.dtype
    return pl.pallas_call(
        return_kernel,
        out_shape=(
            jax.ShapeDtypeStruct((steps * row_count, YS * columns), kept),
            jax.ShapeDtypeStruct((XS * CS, ZS) + scales.shape, scales.dtype),
        ),
        in_specs=[pl.BlockSpec(memory_space=pl.ANY), vmem, vmem],
        out_specs=(vmem, vmem),
        scratch_shapes=[
            pltpu.VMEM((steps, CS * XS, YS, block, columns), kept),
            pltpu.VMEM((steps, ZS, YS * row_count, columns), kept),
            pltpu.VMEM((steps, ZS, YS * row_count, columns), kept),
            pltpu.VMEM((YS, steps * row_count, columns), kept),
            pltpu.VMEM((YS, steps * row_count, columns), kept),
            pltpu.SemaphoreType.DMA((2 * steps + 3,)),
            pltpu.SemaphoreType.DMA((2 * steps + 3,)),
            pltpu.SemaphoreType.DMA((steps,)),
        ],
        compiler_params=pltpu.CompilerParams(
            collective_id=1, has_side_effects=True, vmem_limit_bytes=48 * 1024 * 1024
        ),
        cost_estimate=pl.CostEstimate(flops=20_000_000_000, bytes_accessed=10_000_000, transcendentals=0),
        name="give_back",
    )(outcome, mixing, scales)


def slot_codes(named, base, axis):
    counted = named.astype(jnp.int32)
    return jnp.where(named, base + jnp.cumsum(counted, axis=axis) - counted, -1)


def layer(tokens, route_ids, route_weights, placement, expert_in, expert_down):
    experts = placement.shape[0]
    engines = lax.axis_size("engine")
    peers = lax.axis_size("ep")
    me = lax.axis_index("ep")
    _, _, my_z, _ = place()
    steps, row_count, width = tokens.shape
    capacity = 2
    tops = route_ids.shape[2]
    hidden_units = expert_in.shape[3]
    units = hidden_units // engines
    columns = width // engines
    numbers = jnp.arange(experts, dtype=jnp.int32)

    everyone = lax.all_gather(tokens, "ep", axis=0, tiled=False)
    meta = jnp.concatenate([route_ids.astype(jnp.float32), route_weights], axis=2).reshape(steps * row_count, -1)
    meta = jnp.pad(meta, ((0, 0), (0, 128 - 2 * tops)))
    plane, cols = pass_notes(meta)
    parts = jnp.concatenate([expert_in[..., e * units : (e + 1) * units] for e in range(engines)], axis=0)
    parts, plane = lax.optimization_barrier((parts, plane))
    held_in = lax.all_to_all(parts, BOTH, split_axis=0, concat_axis=0, tiled=True)
    held_down = lax.all_to_all(
        jnp.transpose(expert_down, (0, 2, 1)), "ep", split_axis=0, concat_axis=0, tiled=True
    ).reshape(columns, hidden_units)

    named = jnp.any(plane[..., :tops] == me.astype(jnp.float32), axis=-1)
    named = jnp.transpose(named, (1, 2, 0, 3)).reshape(XS, ZS, CS, steps, row_count)
    at_x = jnp.arange(XS, dtype=jnp.int32)[:, None, None, None, None]
    at_z = jnp.arange(ZS, dtype=jnp.int32)[None, :, None, None, None]
    at_c = jnp.arange(CS, dtype=jnp.int32)[None, None, :, None, None]
    codes = slot_codes(named, ((at_c * XS + at_x) * ZS + at_z) * capacity, 4)
    codes = jnp.transpose(codes, (3, 0, 1, 2, 4)).reshape(steps, peers * row_count)
    slots = jnp.arange(peers * capacity, dtype=jnp.int32)
    arrived = []
    for step in range(steps):
        chosen = (slots[:, None] == codes[step][None, :]).astype(jnp.bfloat16)
        rows = everyone[:, step].reshape(peers * row_count, width)
        arrived.append(jnp.dot(chosen, rows, preferred_element_type=jnp.float32).astype(jnp.bfloat16))
    arrived = jnp.stack(arrived)
    gathered = lax.all_gather(arrived, "engine", axis=1, tiled=True)

    near = jnp.arange(CS * XS, dtype=jnp.int32)
    expert_of = (near % XS) * (ZS * CS) + my_z * CS + near // XS
    ids = jnp.transpose(cols[..., :tops].reshape(YS, ZS, steps, row_count, tops), (2, 1, 0, 3, 4))
    strength = jnp.transpose(cols[..., tops : 2 * tops].reshape(YS, ZS, steps, row_count, tops), (2, 1, 0, 3, 4))
    wanted = ids[..., None] == expert_of.astype(jnp.float32)
    strength = jnp.sum(jnp.where(wanted, strength[..., None], 0.0), axis=4)
    base = near * (YS * ZS) + jnp.arange(YS, dtype=jnp.int32)[None, None, :, None, None] * ZS
    base = (base + jnp.arange(ZS, dtype=jnp.int32)[None, :, None, None, None]) * capacity
    spots = slot_codes(jnp.any(wanted, axis=4), base, 3)
    lanes = jnp.arange(CS * XS * YS * ZS * capacity, dtype=jnp.int32)
    spots = spots.reshape(steps, ZS * YS * row_count, CS * XS)
    strength = strength.reshape(steps, ZS * YS * row_count, CS * XS)
    mixing = sum(
        jnp.where(spots[:, :, n, None] == lanes, strength[:, :, n, None], 0.0) for n in range(CS * XS)
    )

    top = jnp.max(jnp.abs(held_in), axis=(0, 2)).astype(jnp.float32)
    scale_in = (top + EPSILON) / quant_levels
    quant_in = jnp.floor(held_in.astype(jnp.float32) / scale_in[None, :, None, :] + 0.5).astype(jnp.bfloat16)
    quant_in = jnp.transpose(quant_in, (1, 0, 2, 3)).reshape(2, width, units)
    projected = jnp.einsum("snd,mdf->msnf", gathered, quant_in, preferred_element_type=jnp.float32)
    projected = projected * scale_in[:, None, None, :]
    hidden = (jax.nn.silu(projected[0]) * projected[1]).astype(jnp.bfloat16)
    hidden = lax.all_gather(hidden, "engine", axis=0, tiled=False)
    hidden = jnp.concatenate([hidden[e] for e in range(engines)], axis=-1)

    scale_out = (jnp.max(jnp.abs(held_down), axis=1).astype(jnp.float32) + EPSILON) / quant_levels
    quant_down = jnp.floor(held_down.astype(jnp.float32) / scale_out[:, None] + 0.5).astype(jnp.bfloat16)
    summed = jnp.einsum("snf,cf->snc", hidden, quant_down, preferred_element_type=jnp.float32)
    outcome = (summed * scale_out).astype(jnp.bfloat16)
    outcome = outcome.reshape(steps, YS, CS * XS, ZS * capacity, columns)
    scales = jnp.concatenate([scale_in.reshape(-1), scale_out, jnp.zeros((256,), jnp.float32)]).reshape(16, 128)
    combined, heard = give_back(outcome, mixing, scales, row_count)
    mine = jnp.sum(jnp.where(placement == me, numbers, 0))
    spot = ((mine % CS) * XS + mine // (ZS * CS)) * ZS + (mine // CS) % ZS
    picked = lax.dynamic_index_in_dim(heard.reshape(experts, -1), spot, 0, keepdims=False)
    in_scales = picked[: 2 * units].reshape(1, 2, units)
    out_scales = picked[2 * units : 2 * units + columns].reshape(1, columns)
    return (combined.reshape(steps, row_count, width), in_scales, out_scales)


def solution(mesh):
    placed = (
        P(None, ("engine", "ep"), None),
        P(None, ("engine", "ep"), None),
        P(None, ("engine", "ep"), None),
        P(),
        P(None, None, ("engine", "ep"), None),
        P(None, None, ("engine", "ep")),
    )
    return jax.shard_map(
        layer,
        mesh=mesh,
        in_specs=placed,
        out_specs=(P(None, ("engine", "ep"), None), P("ep", None, "engine"), P("ep", "engine")),
        check_vma=False,
    )
```

time: 583 us -> 383 us (0.66)
  Pallas kernels: 143 us -> 81 us
  local copies, waits for them, and re-layouts: 74.2 us -> 12.3 us
  waiting for transfers between devices: 266 us -> 209 us
  other arithmetic: 43.3 us -> 26.3 us
    unnamed x6 -> x3, waiting for transfers between devices: 125 us -> 0.71 us
    all_gather x0 -> x1, waiting for transfers between devices: none -> 94 us  [layer(): everyone = lax.all_gather(tokens, 'ep', axis=0, tiled=False)]
    all_to_all x1, waiting for transfers between devices: 139 us -> 60.3 us  [layer(): lax.all_to_all(parts, BOTH, split_axis=0, concat_axis=0, tiled=True)]
    pallas_call x2, Pallas kernels: 143 us -> 81 us  [the longest x1 59.1 us: give_back(): pl.pallas_call(return_kernel, out_shape=(jax.ShapeDtypeStruct((steps * ro...]
    broadcast_in_dim x9 -> x1, local copies, waits for them, and re-layouts: 36 us -> 0.01 us  [layer(): jnp.zeros((256,), jnp.float32)]
    all_gather x1, waiting for transfers between devices: 0.01 us -> 26 us  [layer(): gathered = lax.all_gather(arrived, 'engine', axis=1, tiled=True)]
    and x1 -> x0, local copies, waits for them, and re-layouts: 20.4 us -> none  [layer(): slots[:, :, :, None, None, :] & blocks[None, :, None, :, None, None]]
    and x5 -> x0, other arithmetic: 15.4 us -> none  [the longest x2 15.2 us: layer(): slots[:, :, :, None, None, :] & blocks[None, :, None, :, None, None]]
  transfers between devices with their start and end apart: 6 -> 5, of which waited for: 3 -> 5; matrix products, arithmetic and copies ran while one was open for 16% -> 13% of each run, Pallas kernels for 8% -> 6%
where the time goes in v3:
time: 383 us; the launch traced here: 382 us
  waiting for transfers between devices  209 us (55%)
  Pallas kernels  81 us (21%)
  other arithmetic  26.3 us (7%)
  matrix products  22.5 us (6%)
  between operations  16.8 us (4%)
  starting transfers between devices  14.4 us (4%)
  local copies, waits for them, and re-layouts  12.3 us (3%)
    all_gather x1, waiting for transfers between devices, layer(): everyone = lax.all_gather(tokens, 'ep', axis=0, tiled=False)  94 us
    all_to_all x1, waiting for transfers between devices, layer(): lax.all_to_all(parts, BOTH, split_axis=0, concat_axis=0, tiled=True)  60.3 us
    pallas_call x1, Pallas kernels, give_back(): pl.pallas_call(return_kernel, out_shape=(jax.ShapeDtypeStruct((steps * ro...  59.1 us
    all_gather x1, waiting for transfers between devices, layer(): gathered = lax.all_gather(arrived, 'engine', axis=1, tiled=True)  26 us
    pallas_call x1, Pallas kernels, pass_notes(): pl.pallas_call(notes_kernel, out_shape=(jax.ShapeDtypeStruct((CS, XS, ZS)...  21.9 us
    all_gather x1, waiting for transfers between devices, layer(): hidden = lax.all_gather(hidden, 'engine', axis=0, tiled=False)  15.3 us
    all_to_all x1, waiting for transfers between devices, layer(): lax.all_to_all(jnp.transpose(expert_down, (0, 2, 1)), 'ep', split_axis=0,...  12.8 us
    dot_general x1, matrix products, layer(): jnp.einsum('snd,mdf->msnf', gathered, quant_in, preferred_element_type=jn...  11.2 us
  transfers between devices with their start and end apart: 5, of which 5 were waited for; matrix products, arithmetic and copies ran while one was open for 13% of the time, Pallas kernels for 6%

profile of v3, /device:TPU:1, one launch (start us, length us, event | category | flops | bytes accessed | tf_op | source)
XLA Modules:
  0.0 382.5 jit_solution(3281960274418045937)
XLA Ops:
  7.2 0.7 all-gather.9.cloned.1.call-update
  7.9 0.7 convert_element_type.79
  8.6 0.8 maximum_bitcast_fusion
  9.4 0.6 pad.4.meta_ref
  10.0 21.9 %notes.1 = (f32[2,4,8,16,128]{4,3,2,1,0:T(8,128)}, f32[4,8,16,128]{3,2,1,0:T(8,128)}) custom-call(f32[16,128]{1,0:T(8,128)} %pad.4.meta_ref), custom_call_target="tpu_custom_call" | custom-call | tf_op jit(solution)/shard_map/notes/pallas_call | solution.py:84
  31.9 3.6 fusion.37
  35.5 3.4 pad_maximum_fusion
  38.9 9.2 %all-to-all-start = ((bf16[256,2,16,384]{3,2,1,0:T(8,128)(2,1)}), bf16[256,2,16,384]{3,2,1,0:T(8,128)(2,1)}, u32[]{:S(2)}, u32[]{:S(2)}) async-start(bf16[256,2,16,384]{3,2,1,0:T(8,128)(2,1)} %pad_maximum_fusion), calls=%async_computation | async-start | bytes 12582912 | tf_op jit(solution)/shard_map/all_to_all | solution.py:207
  48.1 1.2 fusion.27
  50.0 94.0 %all-gather.9.cloned.1.call-done = bf16[128,8,4096]{2,1,0:T(8,128)(2,1)} async-done(((bf16[2,8,4096]{2,1,0:T(8,128)(2,1)}), bf16[128,8,4096]{2,1,0:T(8,128)(2,1)}) %all-gather.9.cloned.1.call-update) | async-done | bytes 8388624 | tf_op jit(solution)/shard_map/all_gather | solution.py:201
  144.0 2.9 fusion.6
  146.9 2.9 fusion.5
  149.8 1.6 pad_maximum_fusion.1
  151.4 60.3 %all-to-all-done = bf16[256,2,16,384]{3,2,1,0:T(8,128)(2,1)} async-done(((bf16[256,2,16,384]{3,2,1,0:T(8,128)(2,1)}), bf16[256,2,16,384]{3,2,1,0:T(8,128)(2,1)}, u32[]{:S(2)}, u32[]{:S(2)}) %all-to-all-start) | async-done | bytes 6291488 | tf_op jit(solution)/shard_map/all_to_all | solution.py:207
  211.7 5.1 %all-to-all-start.1 = ((bf16[64,16,1536]{2,1,0:T(8,128)(2,1)}), bf16[64,16,1536]{2,1,0:T(8,128)(2,1)}, u32[]{:S(2)}, u32[]{:S(2)}) async-start(bf16[64,16,1536]{2,1,0:T(8,128)(2,1)} %bitcast.18), calls=%async_computation.1 | async-start | bytes 6291456 | tf_op jit(solution)/shard_map/all_to_all | solution.py:208
  216.9 3.7 abs_reduce_fusion
  220.6 7.5 %floor_convert_fusion = bf16[256,2,16,384]{3,2,0,1:T(8,128)(2,1)} fusion(bf16[256,2,16,384]{3,2,1,0:T(8,128)(2,1)} %all-to-all-done, f32[2,384]{1,0:T(2,128)S(1)} %add_multiply_fusion.3), kind=kLoop, calls=%fused_computation | loop fusion | flops 15728640 | bytes 12585984 | tf_op jit(solution)/shard_map/convert_element_type | solution.py:246
  228.1 26.0 %all-gather.5.cloned.1.call-done = bf16[2,512,4096]{2,1,0:T(8,128)(2,1)} async-done(((bf16[2,128,4096]{2,1,0:T(8,128)(2,1)}), bf16[2,512,4096]{2,1,0:T(8,128)(2,1)}) %all-gather.5.cloned.1.call-update) | async-done | bytes 8388624 | tf_op jit(solution)/shard_map/all_gather | solution.py:226
  254.1 11.2 %multiply_bitcast_fusion = f32[2,2,512,384]{2,3,1,0:T(8,128)S(1)} fusion(bf16[2,4096,384,1]{2,1,3,0:T(8,128)(2,1)} %bitcast.101, bf16[2,512,4096]{2,1,0:T(8,128)(2,1)} %all-gather.5.cloned.1.call-done, f32[2,384]{1,0:T(2,128)S(1)} %add_multiply_fusion.3), kind=kOutput, calls=%fused_computation.28 | convolution fusion | flops 6443237376 | bytes 17828864 | tf_op jit(solution)/shard_map/snd,mdf->msnf/dot_general | solution.py:248
  265.9 1.1 copy.35
  267.1 0.6 fusion.34
  270.5 1.2 fusion.19
  272.4 0.9 compare_reduce_fusion
  275.1 1.2 select_add_fusion.mixing
  276.2 12.8 %all-to-all-done.1 = bf16[64,16,1536]{2,1,0:T(8,128)(2,1)} async-done(((bf16[64,16,1536]{2,1,0:T(8,128)(2,1)}), bf16[64,16,1536]{2,1,0:T(8,128)(2,1)}, u32[]{:S(2)}, u32[]{:S(2)}) %all-to-all-start.1) | async-done | bytes 3145760 | tf_op jit(solution)/shard_map/all_to_all | solution.py:208
  289.1 2.6 abs_reduce_fusion.1
  291.8 15.3 %all-gather.7.cloned.1.call-done = bf16[4,2,512,384]{3,2,1,0:T(8,128)(2,1)} async-done(((bf16[1,2,512,384]{3,2,1,0:T(8,128)(2,1)}), bf16[4,2,512,384]{3,2,1,0:T(8,128)(2,1)}) %all-gather.7.cloned.1.call-update) | async-done | bytes 3145744 | tf_op jit(solution)/shard_map/all_gather | solution.py:251
  307.1 2.2 slice_bitcast_fusion.7
  309.2 5.4 %multiply_convert_fusion = bf16[2,512,1024]{2,1,0:T(8,128)(2,1)S(1)} fusion(f32[1024]{0:T(1024)S(1)} %div.74, bf16[1024,1536]{1,0:T(8,128)(2,1)} %bitcast.42, bf16[2,512,384]{2,1,0:T(8,128)(2,1)S(1)} %get-tuple-element.20, bf16[2,512,384]{2,1,0:T(8,128)(2,1)S(1)} %get-tuple-element.21, bf16[2,512,384]{2,1,0:T(8,128)(2,1)S(1)} %get-tuple-element.22, ...), kind=kOutput, calls=%fused_computation.15 | convolution fusion | flops 3243769856 | bytes 8392704 | tf_op jit(solution)/shard_map/snf,cf->snc/dot_general | solution.py:256
  314.7 59.1 %give_back.1 = (bf16[16,4096]{1,0:T(8,128)(2,1)S(1)}, f32[8,8,16,128]{3,2,1,0:T(8,128)S(1)}) custom-call(bf16[2,4,8,16,1024]{4,3,2,1,0:T(8,128)(2,1)S(1)} %bitcast.99, f32[2,256,512]{2,1,0:T(8,128)S(1)} %select_add_fusion.mixing, f32[16,128]{1,0:T(8,128)S(1)} %maximum_bitcast_fusion.1.scales), custom_call_target="tpu_custom_call" | custom-call | flops 20000000000 | bytes 10000000 | tf_op jit(solution)/shard_map/give_back/pallas_call | solution.py:156
  374.6 0.7 dynamic-slice.1
  375.3 0.7 copy.87
  (60 shorter events, 4.7 us)
Async XLA Ops:
  7.2 136.9 %all-gather.9.cloned.1.call-start = ((), (), s32[]{:S(2)}) async-start(), calls=%async_computation.4 | async-start | bytes 8519680 | tf_op jit(solution)/shard_map/all_gather | solution.py:201
  38.9 9.2 %copy-start.1 = (f32[2,4,8,16,128]{4,3,2,1,0:T(8,128)S(1)}, f32[2,4,8,16,128]{4,3,2,1,0:T(8,128)}, u32[]{:S(2)}) copy-start(f32[2,4,8,16,128]{4,3,2,1,0:T(8,128)} %get-tuple-element.11) | copy-start | bytes 1572868
  38.9 172.8 %all-to-all-start = ((bf16[256,2,16,384]{3,2,1,0:T(8,128)(2,1)}), bf16[256,2,16,384]{3,2,1,0:T(8,128)(2,1)}, u32[]{:S(2)}, u32[]{:S(2)}) async-start(bf16[256,2,16,384]{3,2,1,0:T(8,128)(2,1)} %pad_maximum_fusion), calls=%async_computation | async-start | bytes 12582912 | tf_op jit(solution)/shard_map/all_to_all | solution.py:207
  48.1 206.0 %all-gather.5.cloned.1.call-start = ((), (), s32[]{:S(2)}) async-start(), calls=%async_computation.2 | async-start | bytes 10485760 | tf_op jit(solution)/shard_map/all_gather | solution.py:226
  211.7 77.3 %all-to-all-start.1 = ((bf16[64,16,1536]{2,1,0:T(8,128)(2,1)}), bf16[64,16,1536]{2,1,0:T(8,128)(2,1)}, u32[]{:S(2)}, u32[]{:S(2)}) async-start(bf16[64,16,1536]{2,1,0:T(8,128)(2,1)} %bitcast.18), calls=%async_computation.1 | async-start | bytes 6291456 | tf_op jit(solution)/shard_map/all_to_all | solution.py:208
  216.9 90.2 %all-gather.7.cloned.1.call-start = ((), (), s32[]{:S(2)}) async-start(), calls=%async_computation.3 | async-start | bytes 3932160 | tf_op jit(solution)/shard_map/all_gather | solution.py:251
  265.4 1.7 copy-start.2
  265.4 5.0 %copy-start = (f32[4,8,16,128]{3,2,1,0:T(8,128)S(1)}, f32[4,8,16,128]{3,2,1,0:T(8,128)}, u32[]{:S(2)}) copy-start(f32[4,8,16,128]{3,2,1,0:T(8,128)} %get-tuple-element.12) | copy-start | bytes 786436
Sparse Core Ops, SparseCore 0:
  10.7 133.2 all-gather.8
  151.5 102.5 all-gather.4
  267.2 39.8 all-gather.6

commit v4 on v3

v4 whole, which is shorter than its diff:
```python
import jax
import jax.numpy as jnp
from jax import lax
from jax.experimental import pallas as pl
from jax.experimental.pallas import tpu as pltpu
from jax.sharding import PartitionSpec as P


EPSILON = 1e-06
quant_levels = 31.0
BOTH = ("engine", "ep")
MESH = pl.DeviceIdType.MESH
XS, ZS, CS, YS = 4, 8, 2, 4


def place():
    p = lax.axis_index("ep")
    return lax.axis_index("engine"), p // (ZS * CS), (p // CS) % ZS, p % CS


def device(y, x, z, c):
    return {"engine": y, "ep": x * (ZS * CS) + z * CS + c}


def peers_of(kind):
    y, x, z, c = place()
    if kind == "z":
        return [device(y, x, (z + d) % ZS, c) for d in (4, 3, 5, 2, 6, 1, 7)]
    if kind == "x":
        return [device(y, (x + d) % XS, z, c) for d in (2, 1, 3)]
    if kind == "y":
        return [device((y + d) % YS, x, z, c) for d in (2, 1, 3)]
    if kind == "c":
        return [device(y, x, z, 1 - c)]
    return [device(y, (x + d) % XS, z, (c + f) % CS) for f in (0, 1) for d in range(XS) if (d, f) != (0, 0)]


def greet(kinds):
    barrier = pltpu.get_barrier_semaphore()
    count = 0
    for kind in kinds:
        for peer in peers_of(kind):
            pl.semaphore_signal(barrier, inc=1, device_id=peer, device_id_type=MESH)
            count += 1
    pl.semaphore_wait(barrier, count)


def send(src, dst, send_sem, recv_sem, peer):
    copy = pltpu.make_async_remote_copy(
        src_ref=src, dst_ref=dst, send_sem=send_sem, recv_sem=recv_sem, device_id=peer, device_id_type=MESH
    )
    copy.start()
    return copy


def await_bytes(like, sem):
    pltpu.make_async_copy(like, like, sem).wait()


def return_kernel(outcome, mixing, scales, out, heard, first, partial, second, total, third, sent, got, own):
    steps, block = mixing.shape[0], first.shape[3]
    y, x, z, c = place()
    here = c * XS + x

    def rows_for(s, peer):
        return outcome.at[:, pl.ds(pl.multiple_of((s * CS * XS + peer) * block, block), block)]

    greet(("xc", "z", "y"))
    locals_ = []
    last = 2 * steps + 1
    heard[here, z] = scales[...]
    for f, d in ((0, 2), (0, 1), (0, 3), (1, 2), (1, 1), (1, 3), (1, 0)):
        peer = device(y, (x + d) % XS, z, (c + f) % CS)
        send(scales, heard.at[here, z], sent.at[last], got.at[last], peer)
    for s in range(steps):
        local = pltpu.make_async_copy(rows_for(s, here), first.at[s, here], own.at[s])
        local.start()
        locals_.append(local)
        for f, d in ((0, 2), (0, 1), (0, 3), (1, 2), (1, 1), (1, 3), (1, 0)):
            there_x, there_c = (x + d) % XS, (c + f) % CS
            src = rows_for(s, there_c * XS + there_x)
            send(src, first.at[s, here], sent.at[s], got.at[s], device(y, there_x, z, there_c))
    for s in range(steps):
        locals_[s].wait()
        await_bytes(first.at[s, pl.ds(0, XS * CS - 1)], got.at[s])
        rows = first[s].reshape(-1, first.shape[-1]).astype(jnp.float32)
        sums = jnp.dot(mixing[s], rows, precision=lax.Precision.HIGHEST, preferred_element_type=jnp.float32)
        partial[s] = sums.astype(partial.dtype).reshape(partial.shape[1:])
        second[s, z] = partial[s, z]
        for d in (4, 3, 5, 2, 6, 1, 7):
            there = (z + d) % ZS
            send(partial.at[s, there], second.at[s, z], sent.at[steps + s], got.at[steps + s], device(y, x, there, c))
    await_bytes(heard.at[pl.ds(0, XS * CS - 1), z], got.at[last])
    for peer in peers_of("z"):
        send(heard.at[:, z], heard.at[:, z], sent.at[last + 1], got.at[last + 1], peer)
    sums = []
    for s in range(steps):
        await_bytes(second.at[s, pl.ds(0, ZS - 1)], got.at[steps + s])
        sums.append(jnp.sum(second[s].astype(jnp.float32), axis=0).reshape(YS, -1, second.shape[-1]))
    total[...] = jnp.concatenate(sums, axis=1).astype(total.dtype)
    third[y] = total[y]
    for d in (2, 1, 3):
        there = (y + d) % YS
        send(total.at[there], third.at[y], sent.at[2 * steps], got.at[2 * steps], device(there, x, z, c))
    await_bytes(third.at[pl.ds(0, YS - 1)], got.at[2 * steps])
    columns = third.shape[-1]
    for e in range(YS):
        out[:, e * columns : (e + 1) * columns] = third[e]
    await_bytes(heard.at[:, pl.ds(0, ZS - 1)], got.at[last + 1])
    await_bytes(heard.at[pl.ds(0, XS * CS - 1), z], sent.at[last])
    await_bytes(heard.at[:, pl.ds(0, ZS - 1)], sent.at[last + 1])
    for s in range(steps):
        await_bytes(first.at[s, pl.ds(0, XS * CS - 1)], sent.at[s])
        await_bytes(second.at[s, pl.ds(0, ZS - 1)], sent.at[steps + s])
    await_bytes(third.at[pl.ds(0, YS - 1)], sent.at[2 * steps])


def give_back(outcome, mixing, scales, row_count, block):
    steps, columns = mixing.shape[0], outcome.shape[-1]
    vmem = pl.BlockSpec(memory_space=pltpu.VMEM)
    kept = outcome.dtype
    return pl.pallas_call(
        return_kernel,
        out_shape=(
            jax.ShapeDtypeStruct((steps * row_count, YS * columns), kept),
            jax.ShapeDtypeStruct((XS * CS, ZS) + scales.shape, scales.dtype),
        ),
        in_specs=[pl.BlockSpec(memory_space=pl.ANY), vmem, vmem],
        out_specs=(vmem, vmem),
        scratch_shapes=[
            pltpu.VMEM((steps, CS * XS, YS, block, columns), kept),
            pltpu.VMEM((steps, ZS, YS * row_count, columns), kept),
            pltpu.VMEM((steps, ZS, YS * row_count, columns), kept),
            pltpu.VMEM((YS, steps * row_count, columns), kept),
            pltpu.VMEM((YS, steps * row_count, columns), kept),
            pltpu.SemaphoreType.DMA((2 * steps + 3,)),
            pltpu.SemaphoreType.DMA((2 * steps + 3,)),
            pltpu.SemaphoreType.DMA((steps,)),
        ],
        compiler_params=pltpu.CompilerParams(
            collective_id=0, has_side_effects=True, vmem_limit_bytes=48 * 1024 * 1024
        ),
        cost_estimate=pl.CostEstimate(flops=20_000_000_000, bytes_accessed=10_000_000, transcendentals=0),
        name="give_back",
    )(outcome, mixing, scales)


def exact_parts(values):
    high = lax.reduce_precision(values, 8, 7)
    middle = lax.reduce_precision(values - high, 8, 7)
    return [part.astype(jnp.bfloat16) for part in (high, middle, values - high - middle)]


def layer(tokens, route_ids, route_weights, placement, expert_in, expert_down):
    experts = placement.shape[0]
    engines = lax.axis_size("engine")
    peers = lax.axis_size("ep")
    me = lax.axis_index("ep")
    _, _, my_z, _ = place()
    steps, row_count, width = tokens.shape
    capacity = 2
    tops = route_ids.shape[2]
    hidden_units = expert_in.shape[3]
    units = hidden_units // engines
    columns = width // engines
    numbers = jnp.arange(experts, dtype=jnp.int32)
    z_groups = [[x * ZS * CS + z * CS + c for z in range(ZS)] for x in range(XS) for c in range(CS)]
    xc_groups = [[x * ZS * CS + z * CS + c for c in range(CS) for x in range(XS)] for z in range(ZS)]

    same = route_ids[:, :, None, :, None] == route_ids[:, None, :, None, :]
    earlier = jnp.arange(row_count)[:, None] > jnp.arange(row_count)[None, :]
    before = jnp.sum((same & earlier[None, :, :, None, None]).astype(jnp.int32), axis=(2, 4))
    marks = (route_ids * capacity + before).astype(jnp.bfloat16)
    notes = jnp.concatenate([marks] + exact_parts(route_weights), axis=2)
    notes = jnp.pad(notes, ((0, 0), (0, 0), (0, 128 - 4 * tops)))
    payload = jnp.concatenate([tokens, notes], axis=2).reshape(steps * row_count, -1)
    column = lax.all_gather(payload, "ep", axis_index_groups=z_groups, axis=0, tiled=False)
    everyone = lax.all_gather(column, "ep", axis_index_groups=xc_groups, axis=0, tiled=False)
    parts = jnp.concatenate([expert_in[..., e * units : (e + 1) * units] for e in range(engines)], axis=0)
    held_in = lax.all_to_all(parts, BOTH, split_axis=0, concat_axis=0, tiled=True)
    held_down = lax.all_to_all(
        jnp.transpose(expert_down, (0, 2, 1)), "ep", split_axis=0, concat_axis=0, tiled=True
    )
    held_down = held_down.reshape(columns, hidden_units)

    marks = everyone[..., width : width + tops].reshape(peers, steps, row_count, tops)
    first = (me * capacity).astype(jnp.bfloat16)
    slot = jnp.where(jnp.any(marks == first, axis=3), 0, jnp.where(jnp.any(marks == first + 1, axis=3), 1, -1))
    base = jnp.arange(peers, dtype=jnp.int32)[:, None, None] * capacity
    base = base + jnp.arange(steps, dtype=jnp.int32)[None, :, None] * (peers * capacity)
    codes = jnp.where(slot >= 0, base + slot, -1).reshape(-1)
    slots = jnp.arange(steps * peers * capacity, dtype=jnp.int32)
    chosen = (slots[:, None] == codes[None, :]).astype(jnp.bfloat16)
    arrived = jnp.dot(
        chosen, everyone.reshape(-1, everyone.shape[-1]), preferred_element_type=jnp.float32
    ).astype(jnp.bfloat16)[:, :width]
    notes = column[..., width : width + 4 * tops].reshape(-1, width)
    notes = jnp.pad(notes, ((0, 8 - notes.shape[0]), (0, 0)))
    gathered = lax.all_gather(jnp.concatenate([arrived, notes]), "engine", axis=0, tiled=False)
    row_total = arrived.shape[0]

    notes = gathered[:, row_total].reshape(YS, ZS, steps, row_count, 4 * tops)
    notes = jnp.transpose(notes, (2, 1, 0, 3, 4)).reshape(steps, ZS * YS * row_count, 4, tops).astype(jnp.float32)
    marks, strength = notes[:, :, 0], notes[:, :, 1] + notes[:, :, 2] + notes[:, :, 3]
    block = jnp.arange(ZS * YS * row_count, dtype=jnp.int32) // row_count
    block = ((block % YS) * ZS + block // YS) * capacity
    lanes = jnp.arange(CS * XS * YS * ZS * capacity, dtype=jnp.int32)
    near = jnp.arange(CS * XS, dtype=jnp.int32)
    target = (((near % XS) * (ZS * CS) + my_z * CS + near // XS) * capacity).astype(jnp.float32)
    lower = marks[..., None] == target
    upper = marks[..., None] == target + 1.0
    share = jnp.sum(jnp.where(lower | upper, strength[..., None], 0.0), axis=2)
    spot = block[:, None] + near * (YS * ZS * capacity) + jnp.any(upper, axis=2).astype(jnp.int32)
    mixing = sum(jnp.where(spot[:, :, n, None] == lanes, share[:, :, n, None], 0.0) for n in range(CS * XS))

    top = jnp.max(jnp.abs(held_in), axis=(0, 2)).astype(jnp.float32)
    scale_in = (top + EPSILON) / quant_levels
    quant_in = jnp.floor(held_in.astype(jnp.float32) / scale_in[None, :, None, :] + 0.5).astype(jnp.bfloat16)
    quant_in = jnp.transpose(quant_in, (1, 0, 2, 3)).reshape(2, width, units)
    rows = gathered.reshape(-1, width)
    projected = jnp.einsum("nd,mdf->mnf", rows, quant_in, preferred_element_type=jnp.float32)
    projected = projected * scale_in[:, None, :]
    hidden = (jax.nn.silu(projected[0]) * projected[1]).astype(jnp.bfloat16)
    hidden = lax.all_gather(hidden, "engine", axis=0, tiled=False)
    hidden = jnp.concatenate([hidden[e] for e in range(engines)], axis=-1)

    scale_out = (jnp.max(jnp.abs(held_down), axis=1).astype(jnp.float32) + EPSILON) / quant_levels
    quant_down = jnp.floor(held_down.astype(jnp.float32) / scale_out[:, None] + 0.5).astype(jnp.bfloat16)
    summed = jnp.einsum("nf,cf->nc", hidden, quant_down, preferred_element_type=jnp.float32)
    outcome = (summed * scale_out).astype(jnp.bfloat16)
    outcome = outcome.reshape(YS, -1, columns)
    scales = jnp.concatenate([scale_in.reshape(-1), scale_out, jnp.zeros((256,), jnp.float32)]).reshape(16, 128)
    combined, heard = give_back(outcome, mixing, scales, row_count, ZS * capacity)
    mine = jnp.sum(jnp.where(placement == me, numbers, 0))
    spot = ((mine % CS) * XS + mine // (ZS * CS)) * ZS + (mine // CS) % ZS
    picked = lax.dynamic_index_in_dim(heard.reshape(experts, -1), spot, 0, keepdims=False)
    in_scales = picked[: 2 * units].reshape(1, 2, units)
    out_scales = picked[2 * units : 2 * units + columns].reshape(1, columns)
    return (combined.reshape(steps, row_count, width), in_scales, out_scales)


def solution(mesh):
    placed = (
        P(None, ("engine", "ep"), None),
        P(None, ("engine", "ep"), None),
        P(None, ("engine", "ep"), None),
        P(),
        P(None, None, ("engine", "ep"), None),
        P(None, None, ("engine", "ep")),
    )
    return jax.shard_map(
        layer,
        mesh=mesh,
        in_specs=placed,
        out_specs=(P(None, ("engine", "ep"), None), P("ep", None, "engine"), P("ep", "engine")),
        check_vma=False,
    )
```

time: 383 us -> 392 us (1.023)
  waiting for transfers between devices: 209 us -> 231 us
  Pallas kernels: 81 us -> 59.2 us
  starting transfers between devices: 14.4 us -> 20.7 us
    pallas_call x1 -> x0, Pallas kernels: 21.9 us -> none  [pass_notes(): pl.pallas_call(notes_kernel, out_shape=(jax.ShapeDtypeStruct((CS, XS, ZS)...]
    all_gather x2 -> x3, waiting for transfers between devices: 120 us -> 138 us  [the longest x1 72.5 us: layer(): lax.all_gather(column, 'ep', axis_index_groups=xc_groups, axis=0, tiled=F...]
    all_to_all x1, starting transfers between devices: 9.16 us -> 16.2 us  [layer(): lax.all_to_all(parts, BOTH, split_axis=0, concat_axis=0, tiled=True)]
    all_to_all x1, waiting for transfers between devices: 12.8 us -> 17.5 us  [layer(): lax.all_to_all(jnp.transpose(expert_down, (0, 2, 1)), 'ep', split_axis=0,...]
    dot_general x4 -> x3, matrix products: 22.5 us -> 20.8 us  [the longest x1 11.1 us: layer(): jnp.einsum('nd,mdf->mnf', rows, quant_in, preferred_element_type=jnp.floa...]
  transfers between devices with their start and end apart: 5 -> 6, of which waited for: 5 -> 6; matrix products, arithmetic and copies ran while one was open for 13% -> 13% of each run, Pallas kernels for 6% -> 0%
where the time goes in v4:
time: 392 us; the launch traced here: 391 us
  waiting for transfers between devices  231 us (59%)
  Pallas kernels  59.2 us (15%)
  other arithmetic  28.2 us (7%)
  matrix products  20.8 us (5%)
  starting transfers between devices  20.7 us (5%)
  between operations  16.8 us (4%)
  local copies, waits for them, and re-layouts  14.3 us (4%)
    all_gather x1, waiting for transfers between devices, layer(): lax.all_gather(column, 'ep', axis_index_groups=xc_groups, axis=0, tiled=F...  72.5 us
    pallas_call x1, Pallas kernels, give_back(): pl.pallas_call(return_kernel, out_shape=(jax.ShapeDtypeStruct((steps * ro...  59.2 us
    all_to_all x1, waiting for transfers between devices, layer(): lax.all_to_all(parts, BOTH, split_axis=0, concat_axis=0, tiled=True)  58.8 us
    all_gather x1, waiting for transfers between devices, layer(): lax.all_gather(payload, 'ep', axis_index_groups=z_groups, axis=0, tiled=F...  37.4 us
    all_gather x1, waiting for transfers between devices, layer(): lax.all_gather(jnp.concatenate([arrived, notes]), 'engine', axis=0, tiled...  28.3 us
    all_to_all x1, waiting for transfers between devices, layer(): lax.all_to_all(jnp.transpose(expert_down, (0, 2, 1)), 'ep', split_axis=0,...  17.5 us
    all_gather x1, waiting for transfers between devices, layer(): hidden = lax.all_gather(hidden, 'engine', axis=0, tiled=False)  16.7 us
    all_to_all x1, starting transfers between devices, layer(): lax.all_to_all(parts, BOTH, split_axis=0, concat_axis=0, tiled=True)  16.2 us
  transfers between devices with their start and end apart: 6, of which 6 were waited for; matrix products, arithmetic and copies ran while one was open for 13% of the time, Pallas kernels for 0%

profile of v4, /device:TPU:1, one launch (start us, length us, event | category | flops | bytes accessed | tf_op | source)
XLA Modules:
  0.0 391.1 jit_solution(14499396996578891729)
XLA Ops:
  7.2 0.7 reduce-precision_convert_fusion.1
  7.9 1.3 convert_reduce_fusion
  9.2 0.7 add_convert_fusion
  10.0 1.6 maximum_bitcast_fusion
  11.6 37.4 %all-gather.7.cloned.1.call-done = bf16[8,16,4224]{2,1,0:T(8,128)(2,1)} async-done(((bf16[1,16,4224]{2,1,0:T(8,128)(2,1)}), bf16[8,16,4224]{2,1,0:T(8,128)(2,1)}) %all-gather.7.cloned.1.call-update) | async-done | bytes 1081360 | tf_op jit(solution)/shard_map/all_gather | solution.py:177
  49.0 3.6 fusion.47
  52.6 3.4 pad_maximum_fusion
  56.0 16.2 %all-to-all-start = ((bf16[256,2,16,384]{3,2,1,0:T(8,128)(2,1)}), bf16[256,2,16,384]{3,2,1,0:T(8,128)(2,1)}, u32[]{:S(2)}, u32[]{:S(2)}) async-start(bf16[256,2,16,384]{3,2,1,0:T(8,128)(2,1)} %pad_maximum_fusion), calls=%async_computation | async-start | bytes 12582912 | tf_op jit(solution)/shard_map/all_to_all | solution.py:180
  72.7 0.8 slice.148
  73.5 72.5 %all-gather.11.cloned.1.call-done = bf16[64,16,4224]{2,1,0:T(8,128)(2,1)} async-done(((bf16[8,16,4224]{2,1,0:T(8,128)(2,1)}), bf16[64,16,4224]{2,1,0:T(8,128)(2,1)}) %all-gather.11.cloned.1.call-update) | async-done | bytes 8650768 | tf_op jit(solution)/shard_map/all_gather | solution.py:178
  146.1 3.2 compare_reduce_fusion
  149.4 5.9 %fusion.25 = bf16[256,4224]{1,0:T(8,128)(2,1)S(1)} fusion(bf16[1024,4224]{1,0:T(8,128)(2,1)} %bitcast.89, s32[1024]{0:T(1024)S(1)} %add_select_fusion), kind=kOutput, calls=%fused_computation.39 | convolution fusion | flops 2214854656 | bytes 10817536 | tf_op jit(solution)/shard_map/dot_general | solution.py:194
  155.6 1.5 fusion.23
  157.1 58.8 %all-to-all-done = bf16[256,2,16,384]{3,2,1,0:T(8,128)(2,1)} async-done(((bf16[256,2,16,384]{3,2,1,0:T(8,128)(2,1)}), bf16[256,2,16,384]{3,2,1,0:T(8,128)(2,1)}, u32[]{:S(2)}, u32[]{:S(2)}) %all-to-all-start) | async-done | bytes 6291488 | tf_op jit(solution)/shard_map/all_to_all | solution.py:180
  215.9 4.3 %all-to-all-start.1 = ((bf16[64,16,1536]{2,1,0:T(8,128)(2,1)}), bf16[64,16,1536]{2,1,0:T(8,128)(2,1)S(1)}, u32[]{:S(2)}, u32[]{:S(2)}) async-start(bf16[64,16,1536]{2,1,0:T(8,128)(2,1)} %bitcast.84), calls=%async_computation.1 | async-start | bytes 6291456 | tf_op jit(solution)/shard_map/all_to_all | solution.py:181
  223.7 3.7 abs_reduce_fusion
  227.4 7.7 %floor_convert_fusion = bf16[256,2,16,384]{3,2,0,1:T(8,128)(2,1)} fusion(bf16[256,2,16,384]{3,2,1,0:T(8,128)(2,1)} %all-to-all-done, f32[2,384]{1,0:T(2,128)S(1)} %add_multiply_fusion.1), kind=kLoop, calls=%fused_computation | loop fusion | flops 15728640 | bytes 12585984 | tf_op jit(solution)/shard_map/convert_element_type | solution.py:218
  235.1 28.3 %all-gather.13.cloned.1.call-done = bf16[1056,4096]{1,0:T(8,128)(2,1)} async-done(((bf16[264,4096]{1,0:T(8,128)(2,1)}), bf16[1056,4096]{1,0:T(8,128)(2,1)}) %all-gather.13.cloned.1.call-update) | async-done | bytes 8650768 | tf_op jit(solution)/shard_map/all_gather | solution.py:199
  263.4 11.1 %fusion.9 = f32[2,1056,384]{2,1,0:T(8,128)S(1)} fusion(bf16[2,4096,384]{2,1,0:T(8,128)(2,1)} %bitcast.83, bf16[1056,4096]{1,0:T(8,128)(2,1)} %all-gather.13.cloned.1.call-done, f32[2,384]{1,0:T(2,128)S(1)} %add_multiply_fusion.1), kind=kOutput, calls=%fused_computation.14 | convolution fusion | flops 6644588544 | bytes 18189312 | tf_op jit(solution)/shard_map/nd,mdf->mnf/dot_general | solution.py:221
  274.6 1.4 fusion.24
  276.0 17.5 %all-to-all-done.1 = bf16[64,16,1536]{2,1,0:T(8,128)(2,1)S(1)} async-done(((bf16[64,16,1536]{2,1,0:T(8,128)(2,1)}), bf16[64,16,1536]{2,1,0:T(8,128)(2,1)S(1)}, u32[]{:S(2)}, u32[]{:S(2)}) %all-to-all-start.1) | async-done | bytes 3145760 | tf_op jit(solution)/shard_map/all_to_all | solution.py:181
  293.5 0.7 abs_reduce_fusion.1
  294.2 0.9 copy-done
  295.2 1.0 slice.155
  296.4 1.0 copy.30
  297.4 1.1 reshape.299
  298.9 1.1 select_add_fusion.mixing
  300.0 16.7 %all-gather.9.cloned.1.call-done = bf16[4,1056,384]{2,1,0:T(8,128)(2,1)} async-done(((bf16[1,1056,384]{2,1,0:T(8,128)(2,1)}), bf16[4,1056,384]{2,1,0:T(8,128)(2,1)}) %all-gather.9.cloned.1.call-update) | async-done | bytes 3244048 | tf_op jit(solution)/shard_map/all_gather | solution.py:224
  316.7 2.3 slice_bitcast_fusion.3
  319.6 3.7 fusion.12
  323.3 59.2 %give_back.1 = (bf16[16,4096]{1,0:T(8,128)(2,1)S(1)}, f32[8,8,16,128]{3,2,1,0:T(8,128)S(1)}) custom-call(bf16[4,264,1024]{2,1,0:T(8,128)(2,1)S(1)} %bitcast.81, f32[2,256,512]{2,1,0:T(8,128)S(1)} %select_add_fusion.mixing, f32[16,128]{1,0:T(8,128)S(1)} %maximum_bitcast_fusion.1.scales), custom_call_target="tpu_custom_call" | custom-call | flops 20000000000 | bytes 10000000 | tf_op jit(solution)/shard_map/give_back/pallas_call | solution.py:122
  383.3 0.7 dynamic-slice.1
  (57 shorter events, 4.3 us)
Async XLA Ops:
  7.2 41.8 %all-gather.7.cloned.1.call-start = ((), (), s32[]{:S(2)}) async-start(), calls=%async_computation.2 | async-start | bytes 1216512 | tf_op jit(solution)/shard_map/all_gather | solution.py:177
  11.6 134.5 %all-gather.11.cloned.1.call-start = ((), (), s32[]{:S(2)}) async-start(), calls=%async_computation.4 | async-start | bytes 9732096 | tf_op jit(solution)/shard_map/all_gather | solution.py:178
  56.0 159.9 %all-to-all-start = ((bf16[256,2,16,384]{3,2,1,0:T(8,128)(2,1)}), bf16[256,2,16,384]{3,2,1,0:T(8,128)(2,1)}, u32[]{:S(2)}, u32[]{:S(2)}) async-start(bf16[256,2,16,384]{3,2,1,0:T(8,128)(2,1)} %pad_maximum_fusion), calls=%async_computation | async-start | bytes 12582912 | tf_op jit(solution)/shard_map/all_to_all | solution.py:180
  72.3 191.1 %all-gather.13.cloned.1.call-start = ((), (), s32[]{:S(2)}) async-start(), calls=%async_computation.5 | async-start | bytes 10813440 | tf_op jit(solution)/shard_map/all_gather | solution.py:199
  157.1 63.2 %copy-start.2 = (s32[64]{0:T(128)S(1)}, s32[64]{0:T(128)}, u32[]{:S(2)}) copy-start(s32[64]{0:T(128)} %param.9) | copy-start | bytes 772
  215.9 77.6 %all-to-all-start.1 = ((bf16[64,16,1536]{2,1,0:T(8,128)(2,1)}), bf16[64,16,1536]{2,1,0:T(8,128)(2,1)S(1)}, u32[]{:S(2)}, u32[]{:S(2)}) async-start(bf16[64,16,1536]{2,1,0:T(8,128)(2,1)} %bitcast.84), calls=%async_computation.1 | async-start | bytes 6291456 | tf_op jit(solution)/shard_map/all_to_all | solution.py:181
  220.2 96.5 %all-gather.9.cloned.1.call-start = ((), (), s32[]{:S(2)}) async-start(), calls=%async_computation.3 | async-start | bytes 4055040 | tf_op jit(solution)/shard_map/all_gather | solution.py:224
  293.5 1.7 copy-start
  316.7 2.9 copy-start.1
Sparse Core Ops, SparseCore 0:
  11.7 37.2 all-gather.6
  50.9 95.1 all-gather.10
  157.3 106.0 all-gather.12
  276.1 40.5 all-gather.8

commit v5 on v4

--- a/solution.py
+++ b/solution.py
@@ -58,67 +58,76 @@
 
 
 def return_kernel(outcome, mixing, scales, out, heard, first, partial, second, total, third, sent, got, own):
-    steps, block = mixing.shape[0], first.shape[3]
+    steps, halves, block, part = mixing.shape[0], first.shape[0], first.shape[4], first.shape[5]
     y, x, z, c = place()
     here = c * XS + x
-
-    def rows_for(s, peer):
-        return outcome.at[:, pl.ds(pl.multiple_of((s * CS * XS + peer) * block, block), block)]
+    note = 2 * steps * halves
+    chunks = [(h, s) for h in range(halves) for s in range(steps)]
+
+    def rows_for(h, s, peer):
+        return outcome.at[s, :, pl.ds(pl.multiple_of(peer * block, block), block), pl.ds(h * part, part)]
 
     greet(("xc", "z", "y"))
-    locals_ = []
-    last = 2 * steps + 1
     heard[here, z] = scales[...]
-    for f, d in ((0, 2), (0, 1), (0, 3), (1, 2), (1, 1), (1, 3), (1, 0)):
-        peer = device(y, (x + d) % XS, z, (c + f) % CS)
-        send(scales, heard.at[here, z], sent.at[last], got.at[last], peer)
-    for s in range(steps):
-        local = pltpu.make_async_copy(rows_for(s, here), first.at[s, here], own.at[s])
-        local.start()
-        locals_.append(local)
-        for f, d in ((0, 2), (0, 1), (0, 3), (1, 2), (1, 1), (1, 3), (1, 0)):
+    own_copies = []
+    for k, (h, s) in enumerate(chunks):
+        own_copies.append(pltpu.make_async_copy(rows_for(h, s, here), first.at[h, s, here], own.at[k]))
+        own_copies[k].start()
+        for f, d in ((0, 2), (1, 2), (0, 1), (0, 3), (1, 1), (1, 3), (1, 0)):
             there_x, there_c = (x + d) % XS, (c + f) % CS
-            src = rows_for(s, there_c * XS + there_x)
-            send(src, first.at[s, here], sent.at[s], got.at[s], device(y, there_x, z, there_c))
-    for s in range(steps):
-        locals_[s].wait()
-        await_bytes(first.at[s, pl.ds(0, XS * CS - 1)], got.at[s])
-        rows = first[s].reshape(-1, first.shape[-1]).astype(jnp.float32)
+            src = rows_for(h, s, there_c * XS + there_x)
+            send(src, first.at[h, s, here], sent.at[k], got.at[k], device(y, there_x, z, there_c))
+        if k == 0:
+            for f, d in ((0, 2), (0, 1), (0, 3), (1, 2), (1, 1), (1, 3), (1, 0)):
+                peer = device(y, (x + d) % XS, z, (c + f) % CS)
+                send(scales, heard.at[here, z], sent.at[note], got.at[note], peer)
+    for k, (h, s) in enumerate(chunks):
+        own_copies[k].wait()
+        await_bytes(first.at[h, s, pl.ds(0, XS * CS - 1)], got.at[k])
+        rows = first[h, s].reshape(-1, part).astype(jnp.float32)
         sums = jnp.dot(mixing[s], rows, precision=lax.Precision.HIGHEST, preferred_element_type=jnp.float32)
-        partial[s] = sums.astype(partial.dtype).reshape(partial.shape[1:])
-        second[s, z] = partial[s, z]
+        partial[h, s] = sums.astype(partial.dtype).reshape(partial.shape[2:])
+        second[h, s, z] = partial[h, s, z]
         for d in (4, 3, 5, 2, 6, 1, 7):
             there = (z + d) % ZS
-            send(partial.at[s, there], second.at[s, z], sent.at[steps + s], got.at[steps + s], device(y, x, there, c))
-    await_bytes(heard.at[pl.ds(0, XS * CS - 1), z], got.at[last])
-    for peer in peers_of("z"):
-        send(heard.at[:, z], heard.at[:, z], sent.at[last + 1], got.at[last + 1], peer)
-    sums = []
-    for s in range(steps):
-        await_bytes(second.at[s, pl.ds(0, ZS - 1)], got.at[steps + s])
-        sums.append(jnp.sum(second[s].astype(jnp.float32), axis=0).reshape(YS, -1, second.shape[-1]))
-    total[...] = jnp.concatenate(sums, axis=1).astype(total.dtype)
-    third[y] = total[y]
-    for d in (2, 1, 3):
-        there = (y + d) % YS
-        send(total.at[there], third.at[y], sent.at[2 * steps], got.at[2 * steps], device(there, x, z, c))
-    await_bytes(third.at[pl.ds(0, YS - 1)], got.at[2 * steps])
-    columns = third.shape[-1]
-    for e in range(YS):
-        out[:, e * columns : (e + 1) * columns] = third[e]
-    await_bytes(heard.at[:, pl.ds(0, ZS - 1)], got.at[last + 1])
-    await_bytes(heard.at[pl.ds(0, XS * CS - 1), z], sent.at[last])
-    await_bytes(heard.at[:, pl.ds(0, ZS - 1)], sent.at[last + 1])
-    for s in range(steps):
-        await_bytes(first.at[s, pl.ds(0, XS * CS - 1)], sent.at[s])
-        await_bytes(second.at[s, pl.ds(0, ZS - 1)], sent.at[steps + s])
-    await_bytes(third.at[pl.ds(0, YS - 1)], sent.at[2 * steps])
-
-
-def give_back(outcome, mixing, scales, row_count, block):
+            pair = note + 3 + k
+            send(partial.at[h, s, there], second.at[h, s, z], sent.at[pair], got.at[pair], device(y, x, there, c))
+        if k == 0:
+            await_bytes(heard.at[pl.ds(0, XS * CS - 1), z], got.at[note])
+            for peer in peers_of("z"):
+                send(heard.at[:, z], heard.at[:, z], sent.at[note + 1], got.at[note + 1], peer)
+    for h in range(halves):
+        sums = []
+        for s in range(steps):
+            await_bytes(second.at[h, s, pl.ds(0, ZS - 1)], got.at[note + 3 + h * steps + s])
+            sums.append(jnp.sum(second[h, s].astype(jnp.float32), axis=0).reshape(YS, -1, part))
+        total[h] = jnp.concatenate(sums, axis=1).astype(total.dtype)
+        third[h, y] = total[h, y]
+        for d in (2, 1, 3):
+            there = (y + d) % YS
+            last = steps * halves + h
+            send(total.at[h, there], third.at[h, y], sent.at[last], got.at[last], device(there, x, z, c))
+    for h in range(halves):
+        await_bytes(third.at[h, pl.ds(0, YS - 1)], got.at[steps * halves + h])
+        for e in range(YS):
+            start = (e * halves + h) * part
+            out[:, start : start + part] = third[h, e]
+    await_bytes(heard.at[:, pl.ds(0, ZS - 1)], got.at[note + 1])
+    await_bytes(heard.at[pl.ds(0, XS * CS - 1), z], sent.at[note])
+    await_bytes(heard.at[:, pl.ds(0, ZS - 1)], sent.at[note + 1])
+    for k, (h, s) in enumerate(chunks):
+        await_bytes(first.at[h, s, pl.ds(0, XS * CS - 1)], sent.at[k])
+        await_bytes(second.at[h, s, pl.ds(0, ZS - 1)], sent.at[note + 3 + k])
+    for h in range(halves):
+        await_bytes(third.at[h, pl.ds(0, YS - 1)], sent.at[steps * halves + h])
+
+
+def give_back(outcome, mixing, scales, row_count, block, halves=2):
     steps, columns = mixing.shape[0], outcome.shape[-1]
+    part = columns // halves
     vmem = pl.BlockSpec(memory_space=pltpu.VMEM)
     kept = outcome.dtype
+    count = 3 * steps * halves + 3
     return pl.pallas_call(
         return_kernel,
         out_shape=(
@@ -128,14 +137,14 @@
         in_specs=[pl.BlockSpec(memory_space=pl.ANY), vmem, vmem],
         out_specs=(vmem, vmem),
         scratch_shapes=[
-            pltpu.VMEM((steps, CS * XS, YS, block, columns), kept),
-            pltpu.VMEM((steps, ZS, YS * row_count, columns), kept),
-            pltpu.VMEM((steps, ZS, YS * row_count, columns), kept),
-            pltpu.VMEM((YS, steps * row_count, columns), kept),
-            pltpu.VMEM((YS, steps * row_count, columns), kept),
-            pltpu.SemaphoreType.DMA((2 * steps + 3,)),
-            pltpu.SemaphoreType.DMA((2 * steps + 3,)),
-            pltpu.SemaphoreType.DMA((steps,)),
+            pltpu.VMEM((halves, steps, CS * XS, YS, block, part), kept),
+            pltpu.VMEM((halves, steps, ZS, YS * row_count, part), kept),
+            pltpu.VMEM((halves, steps, ZS, YS * row_count, part), kept),
+            pltpu.VMEM((halves, YS, steps * row_count, part), kept),
+            pltpu.VMEM((halves, YS, steps * row_count, part), kept),
+            pltpu.SemaphoreType.DMA((count,)),
+            pltpu.SemaphoreType.DMA((count,)),
+            pltpu.SemaphoreType.DMA((steps * halves,)),
         ],
         compiler_params=pltpu.CompilerParams(
             collective_id=0, has_side_effects=True, vmem_limit_bytes=48 * 1024 * 1024
@@ -165,7 +174,8 @@
     columns = width // engines
     numbers = jnp.arange(experts, dtype=jnp.int32)
     z_groups = [[x * ZS * CS + z * CS + c for z in range(ZS)] for x in range(XS) for c in range(CS)]
-    xc_groups = [[x * ZS * CS + z * CS + c for c in range(CS) for x in range(XS)] for z in range(ZS)]
+    pairs_xc = [(x, c) for x in range(XS) for c in range(CS)]
+    xc_groups = [[x * ZS * CS + z * CS + c for x, c in pairs_xc] for z in range(ZS)]
 
     same = route_ids[:, :, None, :, None] == route_ids[:, None, :, None, :]
     earlier = jnp.arange(row_count)[:, None] > jnp.arange(row_count)[None, :]
@@ -186,20 +196,22 @@
     marks = everyone[..., width : width + tops].reshape(peers, steps, row_count, tops)
     first = (me * capacity).astype(jnp.bfloat16)
     slot = jnp.where(jnp.any(marks == first, axis=3), 0, jnp.where(jnp.any(marks == first + 1, axis=3), 1, -1))
-    base = jnp.arange(peers, dtype=jnp.int32)[:, None, None] * capacity
-    base = base + jnp.arange(steps, dtype=jnp.int32)[None, :, None] * (peers * capacity)
-    codes = jnp.where(slot >= 0, base + slot, -1).reshape(-1)
-    slots = jnp.arange(steps * peers * capacity, dtype=jnp.int32)
-    chosen = (slots[:, None] == codes[None, :]).astype(jnp.bfloat16)
-    arrived = jnp.dot(
-        chosen, everyone.reshape(-1, everyone.shape[-1]), preferred_element_type=jnp.float32
-    ).astype(jnp.bfloat16)[:, :width]
+    number = jnp.arange(CS * XS, dtype=jnp.int32)
+    near_x, near_c = number // CS, number % CS
+    base = ((near_c * XS + near_x)[:, None] * ZS + jnp.arange(ZS, dtype=jnp.int32)).reshape(peers, 1, 1) * capacity
+    codes = jnp.where(slot >= 0, base + slot, -1)
+    slots = jnp.arange(peers * capacity, dtype=jnp.int32)
     notes = column[..., width : width + 4 * tops].reshape(-1, width)
     notes = jnp.pad(notes, ((0, 8 - notes.shape[0]), (0, 0)))
-    gathered = lax.all_gather(jnp.concatenate([arrived, notes]), "engine", axis=0, tiled=False)
-    row_total = arrived.shape[0]
-
-    notes = gathered[:, row_total].reshape(YS, ZS, steps, row_count, 4 * tops)
+    all_rows = everyone.reshape(-1, everyone.shape[-1])
+    turn = jnp.arange(steps, dtype=jnp.int32)[None, :, None]
+    gathered = []
+    for step in range(steps):
+        chosen = (slots[:, None] == jnp.where(turn == step, codes, -1).reshape(-1)[None, :]).astype(jnp.bfloat16)
+        arrived = jnp.dot(chosen, all_rows, preferred_element_type=jnp.float32).astype(jnp.bfloat16)[:, :width]
+        gathered.append(lax.all_gather(jnp.concatenate([arrived, notes]), "engine", axis=0, tiled=False))
+
+    notes = gathered[0][:, peers * capacity].reshape(YS, ZS, steps, row_count, 4 * tops)
     notes = jnp.transpose(notes, (2, 1, 0, 3, 4)).reshape(steps, ZS * YS * row_count, 4, tops).astype(jnp.float32)
     marks, strength = notes[:, :, 0], notes[:, :, 1] + notes[:, :, 2] + notes[:, :, 3]
     block = jnp.arange(ZS * YS * row_count, dtype=jnp.int32) // row_count
@@ -217,18 +229,21 @@
     scale_in = (top + EPSILON) / quant_levels
     quant_in = jnp.floor(held_in.astype(jnp.float32) / scale_in[None, :, None, :] + 0.5).astype(jnp.bfloat16)
     quant_in = jnp.transpose(quant_in, (1, 0, 2, 3)).reshape(2, width, units)
-    rows = gathered.reshape(-1, width)
-    projected = jnp.einsum("nd,mdf->mnf", rows, quant_in, preferred_element_type=jnp.float32)
-    projected = projected * scale_in[:, None, :]
-    hidden = (jax.nn.silu(projected[0]) * projected[1]).astype(jnp.bfloat16)
-    hidden = lax.all_gather(hidden, "engine", axis=0, tiled=False)
-    hidden = jnp.concatenate([hidden[e] for e in range(engines)], axis=-1)
+    hidden = []
+    for step in range(steps):
+        rows = gathered[step].reshape(-1, width)
+        projected = jnp.einsum("nd,mdf->mnf", rows, quant_in, preferred_element_type=jnp.float32)
+        projected = projected * scale_in[:, None, :]
+        part = (jax.nn.silu(projected[0]) * projected[1]).astype(jnp.bfloat16)
+        part = lax.all_gather(part, "engine", axis=0, tiled=False)
+        hidden.append(jnp.concatenate([part[e] for e in range(engines)], axis=-1))
+    hidden = jnp.concatenate(hidden)
 
     scale_out = (jnp.max(jnp.abs(held_down), axis=1).astype(jnp.float32) + EPSILON) / quant_levels
     quant_down = jnp.floor(held_down.astype(jnp.float32) / scale_out[:, None] + 0.5).astype(jnp.bfloat16)
     summed = jnp.einsum("nf,cf->nc", hidden, quant_down, preferred_element_type=jnp.float32)
     outcome = (summed * scale_out).astype(jnp.bfloat16)
-    outcome = outcome.reshape(YS, -1, columns)
+    outcome = outcome.reshape(steps, YS, -1, columns)
     scales = jnp.concatenate([scale_in.reshape(-1), scale_out, jnp.zeros((256,), jnp.float32)]).reshape(16, 128)
     combined, heard = give_back(outcome, mixing, scales, row_count, ZS * capacity)
     mine = jnp.sum(jnp.where(placement == me, numbers, 0))

time: 392 us -> 441 us (1.12)
  waiting for transfers between devices: 231 us -> 275 us
  matrix products: 20.8 us -> 26.8 us
    all_gather x1, waiting for transfers between devices: 72.5 us -> 0.01 us  [layer(): lax.all_gather(column, 'ep', axis_index_groups=xc_groups, axis=0, tiled=F...]
    all_to_all x1, waiting for transfers between devices: 58.8 us -> 124 us  [layer(): lax.all_to_all(parts, BOTH, split_axis=0, concat_axis=0, tiled=True)]
    all_to_all x1, waiting for transfers between devices: 17.5 us -> 66.4 us  [layer(): lax.all_to_all(jnp.transpose(expert_down, (0, 2, 1)), 'ep', split_axis=0,...]
    all_gather x1 -> x2, waiting for transfers between devices: 16.7 us -> 45.9 us  [layer(): part = lax.all_gather(part, 'engine', axis=0, tiled=False)]
    all_gather x1 -> x2, waiting for transfers between devices: 28.3 us -> 0.11 us  [layer(): lax.all_gather(jnp.concatenate([arrived, notes]), 'engine', axis=0, tiled...]
    all_to_all x1, starting transfers between devices: 4.31 us -> 12.9 us  [layer(): lax.all_to_all(jnp.transpose(expert_down, (0, 2, 1)), 'ep', split_axis=0,...]
    all_to_all x1, starting transfers between devices: 16.2 us -> 9.11 us  [layer(): lax.all_to_all(parts, BOTH, split_axis=0, concat_axis=0, tiled=True)]
    dot_general x1 -> x2, matrix products: 11.1 us -> 14.8 us  [layer(): jnp.einsum('nd,mdf->mnf', rows, quant_in, preferred_element_type=jnp.floa...]
  transfers between devices with their start and end apart: 6 -> 8, of which waited for: 6 -> 6; matrix products, arithmetic and copies ran while one was open for 13% -> 13% of each run, Pallas kernels for 0% -> 0%
where the time goes in v5:
time: 441 us; the launch traced here: 440 us
  waiting for transfers between devices  275 us (62%)
  Pallas kernels  55 us (12%)
  other arithmetic  28.6 us (6%)
  matrix products  26.8 us (6%)
  starting transfers between devices  22.4 us (5%)
  between operations  17.2 us (4%)
  local copies, waits for them, and re-layouts  14.9 us (3%)
    all_to_all x1, waiting for transfers between devices, layer(): lax.all_to_all(parts, BOTH, split_axis=0, concat_axis=0, tiled=True)  124 us
    all_to_all x1, waiting for transfers between devices, layer(): lax.all_to_all(jnp.transpose(expert_down, (0, 2, 1)), 'ep', split_axis=0,...  66.4 us
    pallas_call x1, Pallas kernels, give_back(): pl.pallas_call(return_kernel, out_shape=(jax.ShapeDtypeStruct((steps * ro...  55 us
    all_gather x2, waiting for transfers between devices, layer(): part = lax.all_gather(part, 'engine', axis=0, tiled=False)  45.9 us
    all_gather x1, waiting for transfers between devices, layer(): lax.all_gather(payload, 'ep', axis_index_groups=z_groups, axis=0, tiled=F...  37.4 us
    dot_general x2, matrix products, layer(): jnp.einsum('nd,mdf->mnf', rows, quant_in, preferred_element_type=jnp.floa...  14.8 us
    all_to_all x1, starting transfers between devices, layer(): lax.all_to_all(jnp.transpose(expert_down, (0, 2, 1)), 'ep', split_axis=0,...  12.9 us
    all_to_all x1, starting transfers between devices, layer(): lax.all_to_all(parts, BOTH, split_axis=0, concat_axis=0, tiled=True)  9.11 us
  transfers between devices with their start and end apart: 8, of which 6 were waited for; matrix products, arithmetic and copies ran while one was open for 13% of the time, Pallas kernels for 0%

profile of v5, /device:TPU:1, one launch (start us, length us, event | category | flops | bytes accessed | tf_op | source)
XLA Modules:
  0.0 439.8 jit_solution(13749314480925589528)
XLA Ops:
  7.9 1.3 convert_reduce_fusion
  9.2 0.7 add_convert_fusion
  10.0 1.6 maximum_bitcast_fusion
  11.6 37.4 %all-gather.10.cloned.1.call-done = bf16[8,16,4224]{2,1,0:T(8,128)(2,1)} async-done(((bf16[1,16,4224]{2,1,0:T(8,128)(2,1)}), bf16[8,16,4224]{2,1,0:T(8,128)(2,1)}) %all-gather.10.cloned.1.call-update) | async-done | bytes 1081360 | tf_op jit(solution)/shard_map/all_gather | solution.py:187
  49.0 12.9 %all-to-all-start.1 = ((bf16[64,16,1536]{2,1,0:T(8,128)(2,1)}), bf16[64,16,1536]{2,1,0:T(8,128)(2,1)S(1)}, u32[]{:S(2)}, u32[]{:S(2)}) async-start(bf16[64,16,1536]{2,1,0:T(8,128)(2,1)} %bitcast.105), calls=%async_computation.1 | async-start | bytes 6291456 | tf_op jit(solution)/shard_map/all_to_all | solution.py:191
  61.9 3.6 fusion.60
  65.5 3.5 pad_maximum_fusion
  68.9 66.4 %all-to-all-done.1 = bf16[64,16,1536]{2,1,0:T(8,128)(2,1)S(1)} async-done(((bf16[64,16,1536]{2,1,0:T(8,128)(2,1)}), bf16[64,16,1536]{2,1,0:T(8,128)(2,1)S(1)}, u32[]{:S(2)}, u32[]{:S(2)}) %all-to-all-start.1) | async-done | bytes 3145760 | tf_op jit(solution)/shard_map/all_to_all | solution.py:191
  135.4 9.1 %all-to-all-start = ((bf16[256,2,16,384]{3,2,1,0:T(8,128)(2,1)}), bf16[256,2,16,384]{3,2,1,0:T(8,128)(2,1)}, u32[]{:S(2)}, u32[]{:S(2)}) async-start(bf16[256,2,16,384]{3,2,1,0:T(8,128)(2,1)} %pad_maximum_fusion), calls=%async_computation | async-start | bytes 12582912 | tf_op jit(solution)/shard_map/all_to_all | solution.py:190
  145.4 0.8 slice.176
  146.3 3.3 compare_reduce_fusion
  149.7 4.9 %fusion.35 = bf16[128,4224]{1,0:T(8,128)(2,1)S(1)} fusion(bf16[1024,4224]{1,0:T(8,128)(2,1)} %bitcast.98, s32[1024]{0:T(1024)S(1)} %get-tuple-element.41), kind=kOutput, calls=%fused_computation.56 | convolution fusion | flops 1107427328 | bytes 9736192 | tf_op jit(solution)/shard_map/dot_general | solution.py:211
  154.8 0.8 slice-done.2
  155.6 1.3 fusion.36
  157.1 1.6 fusion.31
  163.7 124.5 %all-to-all-done = bf16[256,2,16,384]{3,2,1,0:T(8,128)(2,1)} async-done(((bf16[256,2,16,384]{3,2,1,0:T(8,128)(2,1)}), bf16[256,2,16,384]{3,2,1,0:T(8,128)(2,1)}, u32[]{:S(2)}, u32[]{:S(2)}) %all-to-all-start) | async-done | bytes 6291488 | tf_op jit(solution)/shard_map/all_to_all | solution.py:190
  288.2 3.6 abs_reduce_fusion
  291.9 7.4 %floor_convert_fusion = bf16[256,2,16,384]{3,2,0,1:T(8,128)(2,1)} fusion(bf16[256,2,16,384]{3,2,1,0:T(8,128)(2,1)} %all-to-all-done, f32[2,384]{1,0:T(2,128)S(1)} %add_multiply_fusion.2), kind=kLoop, calls=%fused_computation | loop fusion | flops 15728640 | bytes 12585984 | tf_op jit(solution)/shard_map/convert_element_type | solution.py:230
  299.3 7.3 %multiply_bitcast_fusion = f32[2,544,384]{2,1,0:T(8,128)S(1)} fusion(bf16[2,4096,384]{2,1,0:T(8,128)(2,1)} %bitcast.103, bf16[544,4096]{1,0:T(8,128)(2,1)} %all-gather.20.cloned.1.call-done, f32[2,384]{1,0:T(2,128)S(1)} %add_multiply_fusion.2), kind=kOutput, calls=%fused_computation.35 | convolution fusion | flops 3422969856 | bytes 12422144 | tf_op jit(solution)/shard_map/nd,mdf->mnf/dot_general | solution.py:235
  306.6 1.0 fusion.33
  307.8 1.0 slice.190
  309.0 1.0 copy.30
  310.0 1.1 reshape.344
  311.3 7.5 %multiply_bitcast_fusion.1 = f32[2,544,384]{2,1,0:T(8,128)S(1)} fusion(bf16[2,4096,384]{2,1,0:T(8,128)(2,1)} %bitcast.104, bf16[544,4096]{1,0:T(8,128)(2,1)} %all-gather.18.cloned.1.call-done, f32[2,384]{1,0:T(2,128)S(1)} %add_multiply_fusion.2), kind=kOutput, calls=%fused_computation.36 | convolution fusion | flops 3422969856 | bytes 12422144 | tf_op jit(solution)/shard_map/nd,mdf->mnf/dot_general | solution.py:235
  318.8 1.0 fusion.34
  320.0 1.1 select_add_fusion.mixing
  321.2 16.0 %all-gather.14.cloned.1.call-done = bf16[4,544,384]{2,1,0:T(8,128)(2,1)} async-done(((bf16[1,544,384]{2,1,0:T(8,128)(2,1)}), bf16[4,544,384]{2,1,0:T(8,128)(2,1)}) %all-gather.14.cloned.1.call-update) | async-done | bytes 1671184 | tf_op jit(solution)/shard_map/all_gather | solution.py:238
  337.1 1.5 slice_bitcast_fusion.3
  338.7 29.9 %all-gather.12.cloned.1.call-done = bf16[4,544,384]{2,1,0:T(8,128)(2,1)} async-done(((bf16[1,544,384]{2,1,0:T(8,128)(2,1)}), bf16[4,544,384]{2,1,0:T(8,128)(2,1)}) %all-gather.12.cloned.1.call-update) | async-done | bytes 1671184 | tf_op jit(solution)/shard_map/all_gather | solution.py:238
  368.6 1.5 slice_bitcast_fusion.7
  370.1 5.7 %fusion.7 = bf16[1088,1024]{1,0:T(8,128)(2,1)S(1)} fusion(bf16[544,384]{1,0:T(8,128)(2,1)S(1)} %get-tuple-element.18, bf16[544,384]{1,0:T(8,128)(2,1)S(1)} %get-tuple-element.19, bf16[544,384]{1,0:T(8,128)(2,1)S(1)} %get-tuple-element.20, bf16[544,384]{1,0:T(8,128)(2,1)S(1)} %get-tuple-element.17, bf16[544,384]{1,0:T(8,128)(2,1)S(1)} %get-tuple-element.14, ...), kind=kOutput, calls=%fused_computation.12 | convolution fusion | flops 3459383296 | bytes 8720384 | tf_op jit(solution)/shard_map/nf,cf->nc/dot_general | solution.py:244
  375.9 55.0 %give_back.1 = (bf16[16,4096]{1,0:T(8,128)(2,1)S(1)}, f32[8,8,16,128]{3,2,1,0:T(8,128)S(1)}) custom-call(bf16[2,4,136,1024]{3,2,1,0:T(8,128)(2,1)S(1)} %bitcast.96, f32[2,256,512]{2,1,0:T(8,128)S(1)} %select_add_fusion.mixing, f32[16,128]{1,0:T(8,128)S(1)} %maximum_bitcast_fusion.1.scales), custom_call_target="tpu_custom_call" | custom-call | flops 20000000000 | bytes 10000000 | tf_op jit(solution)/shard_map/give_back/pallas_call | solution.py:131
  (79 shorter events, 7.2 us)
Async XLA Ops:
  7.2 41.8 %all-gather.10.cloned.1.call-start = ((), (), s32[]{:S(2)}) async-start(), calls=%async_computation.2 | async-start | bytes 1216512 | tf_op jit(solution)/shard_map/all_gather | solution.py:187
  11.6 134.7 %all-gather.16.cloned.1.call-start = ((), (), s32[]{:S(2)}) async-start(), calls=%async_computation.5 | async-start | bytes 9732096 | tf_op jit(solution)/shard_map/all_gather | solution.py:188
  49.0 86.3 %all-to-all-start.1 = ((bf16[64,16,1536]{2,1,0:T(8,128)(2,1)}), bf16[64,16,1536]{2,1,0:T(8,128)(2,1)S(1)}, u32[]{:S(2)}, u32[]{:S(2)}) async-start(bf16[64,16,1536]{2,1,0:T(8,128)(2,1)} %bitcast.105), calls=%async_computation.1 | async-start | bytes 6291456 | tf_op jit(solution)/shard_map/all_to_all | solution.py:191
  135.4 27.6 %copy-start = (bf16[64,16,1536]{2,1,0:T(8,128)(2,1)}, bf16[64,16,1536]{2,1,0:T(8,128)(2,1)S(1)}, u32[]{:S(2)}) copy-start(bf16[64,16,1536]{2,1,0:T(8,128)(2,1)S(1)} %all-to-all-done.1) | copy-start | bytes 9437188
  135.4 152.8 %all-to-all-start = ((bf16[256,2,16,384]{3,2,1,0:T(8,128)(2,1)}), bf16[256,2,16,384]{3,2,1,0:T(8,128)(2,1)}, u32[]{:S(2)}, u32[]{:S(2)}) async-start(bf16[256,2,16,384]{3,2,1,0:T(8,128)(2,1)} %pad_maximum_fusion), calls=%async_computation | async-start | bytes 12582912 | tf_op jit(solution)/shard_map/all_to_all | solution.py:190
  144.5 154.8 %all-gather.20.cloned.1.call-start = ((), (), s32[]{:S(2)}) async-start(), calls=%async_computation.7 | async-start | bytes 5570560 | tf_op jit(solution)/shard_map/all_gather | solution.py:212
  146.3 8.5 %slice-start = ((s8[8650752]{0:T(1024)(128)(4,1)}), s8[262144]{0:T(1024)(128)(4,1)S(1)}, s32[]{:S(2)}) async-start(s8[8650752]{0:T(1024)(128)(4,1)} %bitcast.99), calls=%async_computation.8 | async-start | bytes 524288
  149.7 5.1 %slice-start.1 = ((s8[8650752]{0:T(1024)(128)(4,1)}), s8[4194304]{0:T(1024)(128)(4,1)S(1)}, s32[]{:S(2)}) async-start(s8[8650752]{0:T(1024)(128)(4,1)} %bitcast.99), calls=%async_computation.9 | async-start | bytes 8388608
  149.7 5.9 %slice-start.2 = ((s8[8650752]{0:T(1024)(128)(4,1)}), s8[4194304]{0:T(1024)(128)(4,1)S(1)}, s32[]{:S(2)}) async-start(s8[8650752]{0:T(1024)(128)(4,1)} %bitcast.99), calls=%async_computation.10 | async-start | bytes 8388608
  156.9 2.6 copy-start.1
  158.7 149.1 %all-gather.18.cloned.1.call-start = ((), (), s32[]{:S(2)}) async-start(), calls=%async_computation.6 | async-start | bytes 5570560 | tf_op jit(solution)/shard_map/all_gather | solution.py:212
  159.2 177.9 %all-gather.14.cloned.1.call-start = ((), (), s32[]{:S(2)}) async-start(), calls=%async_computation.4 | async-start | bytes 2088960 | tf_op jit(solution)/shard_map/all_gather | solution.py:238
  307.6 61.0 %all-gather.12.cloned.1.call-start = ((), (), s32[]{:S(2)}) async-start(), calls=%async_computation.3 | async-start | bytes 2088960 | tf_op jit(solution)/shard_map/all_gather | solution.py:238
Sparse Core Ops, SparseCore 0:
  11.7 37.2 all-gather.9
  50.8 85.6 all-gather.15
  158.8 82.0 all-gather.19
  242.5 65.2 all-gather.17
  309.4 27.6 all-gather.13
  338.8 29.7 all-gather.11

commit v6 on v5

--- a/solution.py
+++ b/solution.py
@@ -65,7 +65,8 @@
     chunks = [(h, s) for h in range(halves) for s in range(steps)]
 
     def rows_for(h, s, peer):
-        return outcome.at[s, :, pl.ds(pl.multiple_of(peer * block, block), block), pl.ds(h * part, part)]
+        start = pl.multiple_of((s * CS * XS + peer) * block, block)
+        return outcome.at[:, pl.ds(start, block), pl.ds(h * part, part)]
 
     greet(("xc", "z", "y"))
     heard[here, z] = scales[...]
@@ -174,8 +175,7 @@
     columns = width // engines
     numbers = jnp.arange(experts, dtype=jnp.int32)
     z_groups = [[x * ZS * CS + z * CS + c for z in range(ZS)] for x in range(XS) for c in range(CS)]
-    pairs_xc = [(x, c) for x in range(XS) for c in range(CS)]
-    xc_groups = [[x * ZS * CS + z * CS + c for x, c in pairs_xc] for z in range(ZS)]
+    xc_groups = [[x * ZS * CS + z * CS + c for c in range(CS) for x in range(XS)] for z in range(ZS)]
 
     same = route_ids[:, :, None, :, None] == route_ids[:, None, :, None, :]
     earlier = jnp.arange(row_count)[:, None] > jnp.arange(row_count)[None, :]
@@ -196,22 +196,20 @@
     marks = everyone[..., width : width + tops].reshape(peers, steps, row_count, tops)
     first = (me * capacity).astype(jnp.bfloat16)
     slot = jnp.where(jnp.any(marks == first, axis=3), 0, jnp.where(jnp.any(marks == first + 1, axis=3), 1, -1))
-    number = jnp.arange(CS * XS, dtype=jnp.int32)
-    near_x, near_c = number // CS, number % CS
-    base = ((near_c * XS + near_x)[:, None] * ZS + jnp.arange(ZS, dtype=jnp.int32)).reshape(peers, 1, 1) * capacity
-    codes = jnp.where(slot >= 0, base + slot, -1)
-    slots = jnp.arange(peers * capacity, dtype=jnp.int32)
+    base = jnp.arange(peers, dtype=jnp.int32)[:, None, None] * capacity
+    base = base + jnp.arange(steps, dtype=jnp.int32)[None, :, None] * (peers * capacity)
+    codes = jnp.where(slot >= 0, base + slot, -1).reshape(-1)
+    slots = jnp.arange(steps * peers * capacity, dtype=jnp.int32)
+    chosen = (slots[:, None] == codes[None, :]).astype(jnp.bfloat16)
+    arrived = jnp.dot(
+        chosen, everyone.reshape(-1, everyone.shape[-1]), preferred_element_type=jnp.float32
+    ).astype(jnp.bfloat16)[:, :width]
     notes = column[..., width : width + 4 * tops].reshape(-1, width)
     notes = jnp.pad(notes, ((0, 8 - notes.shape[0]), (0, 0)))
-    all_rows = everyone.reshape(-1, everyone.shape[-1])
-    turn = jnp.arange(steps, dtype=jnp.int32)[None, :, None]
-    gathered = []
-    for step in range(steps):
-        chosen = (slots[:, None] == jnp.where(turn == step, codes, -1).reshape(-1)[None, :]).astype(jnp.bfloat16)
-        arrived = jnp.dot(chosen, all_rows, preferred_element_type=jnp.float32).astype(jnp.bfloat16)[:, :width]
-        gathered.append(lax.all_gather(jnp.concatenate([arrived, notes]), "engine", axis=0, tiled=False))
-
-    notes = gathered[0][:, peers * capacity].reshape(YS, ZS, steps, row_count, 4 * tops)
+    gathered = lax.all_gather(jnp.concatenate([arrived, notes]), "engine", axis=0, tiled=False)
+    row_total = arrived.shape[0]
+
+    notes = gathered[:, row_total].reshape(YS, ZS, steps, row_count, 4 * tops)
     notes = jnp.transpose(notes, (2, 1, 0, 3, 4)).reshape(steps, ZS * YS * row_count, 4, tops).astype(jnp.float32)
     marks, strength = notes[:, :, 0], notes[:, :, 1] + notes[:, :, 2] + notes[:, :, 3]
     block = jnp.arange(ZS * YS * row_count, dtype=jnp.int32) // row_count
@@ -229,21 +227,18 @@
     scale_in = (top + EPSILON) / quant_levels
     quant_in = jnp.floor(held_in.astype(jnp.float32) / scale_in[None, :, None, :] + 0.5).astype(jnp.bfloat16)
     quant_in = jnp.transpose(quant_in, (1, 0, 2, 3)).reshape(2, width, units)
-    hidden = []
-    for step in range(steps):
-        rows = gathered[step].reshape(-1, width)
-        projected = jnp.einsum("nd,mdf->mnf", rows, quant_in, preferred_element_type=jnp.float32)
-        projected = projected * scale_in[:, None, :]
-        part = (jax.nn.silu(projected[0]) * projected[1]).astype(jnp.bfloat16)
-        part = lax.all_gather(part, "engine", axis=0, tiled=False)
-        hidden.append(jnp.concatenate([part[e] for e in range(engines)], axis=-1))
-    hidden = jnp.concatenate(hidden)
+    rows = gathered.reshape(-1, width)
+    projected = jnp.einsum("nd,mdf->mnf", rows, quant_in, preferred_element_type=jnp.float32)
+    projected = projected * scale_in[:, None, :]
+    hidden = (jax.nn.silu(projected[0]) * projected[1]).astype(jnp.bfloat16)
+    hidden = lax.all_gather(hidden, "engine", axis=0, tiled=False)
+    hidden = jnp.concatenate([hidden[e] for e in range(engines)], axis=-1)
 
     scale_out = (jnp.max(jnp.abs(held_down), axis=1).astype(jnp.float32) + EPSILON) / quant_levels
     quant_down = jnp.floor(held_down.astype(jnp.float32) / scale_out[:, None] + 0.5).astype(jnp.bfloat16)
     summed = jnp.einsum("nf,cf->nc", hidden, quant_down, preferred_element_type=jnp.float32)
     outcome = (summed * scale_out).astype(jnp.bfloat16)
-    outcome = outcome.reshape(steps, YS, -1, columns)
+    outcome = outcome.reshape(YS, -1, columns)
     scales = jnp.concatenate([scale_in.reshape(-1), scale_out, jnp.zeros((256,), jnp.float32)]).reshape(16, 128)
     combined, heard = give_back(outcome, mixing, scales, row_count, ZS * capacity)
     mine = jnp.sum(jnp.where(placement == me, numbers, 0))

time: 441 us -> 388 us (0.88)
  waiting for transfers between devices: 275 us -> 231 us
  matrix products: 26.8 us -> 20.8 us
    all_gather x1, waiting for transfers between devices: 0.01 us -> 72.5 us  [layer(): lax.all_gather(column, 'ep', axis_index_groups=xc_groups, axis=0, tiled=F...]
    all_to_all x1, waiting for transfers between devices: 124 us -> 58.8 us  [layer(): lax.all_to_all(parts, BOTH, split_axis=0, concat_axis=0, tiled=True)]
    all_to_all x1, waiting for transfers between devices: 66.4 us -> 17.5 us  [layer(): lax.all_to_all(jnp.transpose(expert_down, (0, 2, 1)), 'ep', split_axis=0,...]
    all_gather x2 -> x1, waiting for transfers between devices: 45.9 us -> 16.7 us  [layer(): hidden = lax.all_gather(hidden, 'engine', axis=0, tiled=False)]
    all_gather x2 -> x1, waiting for transfers between devices: 0.11 us -> 28.3 us  [layer(): lax.all_gather(jnp.concatenate([arrived, notes]), 'engine', axis=0, tiled...]
    all_to_all x1, starting transfers between devices: 12.9 us -> 4.31 us  [layer(): lax.all_to_all(jnp.transpose(expert_down, (0, 2, 1)), 'ep', split_axis=0,...]
    all_to_all x1, starting transfers between devices: 9.11 us -> 16.2 us  [layer(): lax.all_to_all(parts, BOTH, split_axis=0, concat_axis=0, tiled=True)]
    dot_general x2 -> x1, matrix products: 14.8 us -> 11.1 us  [layer(): jnp.einsum('nd,mdf->mnf', rows, quant_in, preferred_element_type=jnp.floa...]
  transfers between devices with their start and end apart: 8 -> 6, of which waited for: 6 -> 6; matrix products, arithmetic and copies ran while one was open for 13% -> 13% of each run, Pallas kernels for 0% -> 0%
where the time goes in v6:
time: 388 us; the launch traced here: 387 us
  waiting for transfers between devices  231 us (60%)
  Pallas kernels  55 us (14%)
  other arithmetic  28.2 us (7%)
  matrix products  20.8 us (5%)
  starting transfers between devices  20.7 us (5%)
  between operations  16.8 us (4%)
  local copies, waits for them, and re-layouts  14.3 us (4%)
    all_gather x1, waiting for transfers between devices, layer(): lax.all_gather(column, 'ep', axis_index_groups=xc_groups, axis=0, tiled=F...  72.5 us
    all_to_all x1, waiting for transfers between devices, layer(): lax.all_to_all(parts, BOTH, split_axis=0, concat_axis=0, tiled=True)  58.8 us
    pallas_call x1, Pallas kernels, give_back(): pl.pallas_call(return_kernel, out_shape=(jax.ShapeDtypeStruct((steps * ro...  55 us
    all_gather x1, waiting for transfers between devices, layer(): lax.all_gather(payload, 'ep', axis_index_groups=z_groups, axis=0, tiled=F...  37.4 us
    all_gather x1, waiting for transfers between devices, layer(): lax.all_gather(jnp.concatenate([arrived, notes]), 'engine', axis=0, tiled...  28.3 us
    all_to_all x1, waiting for transfers between devices, layer(): lax.all_to_all(jnp.transpose(expert_down, (0, 2, 1)), 'ep', split_axis=0,...  17.5 us
    all_gather x1, waiting for transfers between devices, layer(): hidden = lax.all_gather(hidden, 'engine', axis=0, tiled=False)  16.7 us
    all_to_all x1, starting transfers between devices, layer(): lax.all_to_all(parts, BOTH, split_axis=0, concat_axis=0, tiled=True)  16.2 us
  transfers between devices with their start and end apart: 6, of which 6 were waited for; matrix products, arithmetic and copies ran while one was open for 13% of the time, Pallas kernels for 0%

profile of v6, /device:TPU:1, one launch (start us, length us, event | category | flops | bytes accessed | tf_op | source)
XLA Modules:
  0.0 387.0 jit_solution(15703502516156709097)
XLA Ops:
  7.2 0.7 reduce-precision_convert_fusion.1
  7.9 1.3 convert_reduce_fusion
  9.2 0.7 add_convert_fusion
  10.0 1.6 maximum_bitcast_fusion
  11.6 37.4 %all-gather.7.cloned.1.call-done = bf16[8,16,4224]{2,1,0:T(8,128)(2,1)} async-done(((bf16[1,16,4224]{2,1,0:T(8,128)(2,1)}), bf16[8,16,4224]{2,1,0:T(8,128)(2,1)}) %all-gather.7.cloned.1.call-update) | async-done | bytes 1081360 | tf_op jit(solution)/shard_map/all_gather | solution.py:187
  49.0 3.6 fusion.47
  52.6 3.4 pad_maximum_fusion
  56.0 16.2 %all-to-all-start = ((bf16[256,2,16,384]{3,2,1,0:T(8,128)(2,1)}), bf16[256,2,16,384]{3,2,1,0:T(8,128)(2,1)}, u32[]{:S(2)}, u32[]{:S(2)}) async-start(bf16[256,2,16,384]{3,2,1,0:T(8,128)(2,1)} %pad_maximum_fusion), calls=%async_computation | async-start | bytes 12582912 | tf_op jit(solution)/shard_map/all_to_all | solution.py:190
  72.7 0.8 slice.148
  73.5 72.5 %all-gather.11.cloned.1.call-done = bf16[64,16,4224]{2,1,0:T(8,128)(2,1)} async-done(((bf16[8,16,4224]{2,1,0:T(8,128)(2,1)}), bf16[64,16,4224]{2,1,0:T(8,128)(2,1)}) %all-gather.11.cloned.1.call-update) | async-done | bytes 8650768 | tf_op jit(solution)/shard_map/all_gather | solution.py:188
  146.1 3.2 compare_reduce_fusion
  149.4 5.9 %fusion.25 = bf16[256,4224]{1,0:T(8,128)(2,1)S(1)} fusion(bf16[1024,4224]{1,0:T(8,128)(2,1)} %bitcast.89, s32[1024]{0:T(1024)S(1)} %add_select_fusion), kind=kOutput, calls=%fused_computation.39 | convolution fusion | flops 2214854656 | bytes 10817536 | tf_op jit(solution)/shard_map/dot_general | solution.py:204
  155.6 1.5 fusion.23
  157.1 58.8 %all-to-all-done = bf16[256,2,16,384]{3,2,1,0:T(8,128)(2,1)} async-done(((bf16[256,2,16,384]{3,2,1,0:T(8,128)(2,1)}), bf16[256,2,16,384]{3,2,1,0:T(8,128)(2,1)}, u32[]{:S(2)}, u32[]{:S(2)}) %all-to-all-start) | async-done | bytes 6291488 | tf_op jit(solution)/shard_map/all_to_all | solution.py:190
  215.9 4.3 %all-to-all-start.1 = ((bf16[64,16,1536]{2,1,0:T(8,128)(2,1)}), bf16[64,16,1536]{2,1,0:T(8,128)(2,1)S(1)}, u32[]{:S(2)}, u32[]{:S(2)}) async-start(bf16[64,16,1536]{2,1,0:T(8,128)(2,1)} %bitcast.84), calls=%async_computation.1 | async-start | bytes 6291456 | tf_op jit(solution)/shard_map/all_to_all | solution.py:191
  223.7 3.7 abs_reduce_fusion
  227.4 7.7 %floor_convert_fusion = bf16[256,2,16,384]{3,2,0,1:T(8,128)(2,1)} fusion(bf16[256,2,16,384]{3,2,1,0:T(8,128)(2,1)} %all-to-all-done, f32[2,384]{1,0:T(2,128)S(1)} %add_multiply_fusion.1), kind=kLoop, calls=%fused_computation | loop fusion | flops 15728640 | bytes 12585984 | tf_op jit(solution)/shard_map/convert_element_type | solution.py:228
  235.1 28.3 %all-gather.13.cloned.1.call-done = bf16[1056,4096]{1,0:T(8,128)(2,1)} async-done(((bf16[264,4096]{1,0:T(8,128)(2,1)}), bf16[1056,4096]{1,0:T(8,128)(2,1)}) %all-gather.13.cloned.1.call-update) | async-done | bytes 8650768 | tf_op jit(solution)/shard_map/all_gather | solution.py:209
  263.4 11.1 %fusion.9 = f32[2,1056,384]{2,1,0:T(8,128)S(1)} fusion(bf16[2,4096,384]{2,1,0:T(8,128)(2,1)} %bitcast.83, bf16[1056,4096]{1,0:T(8,128)(2,1)} %all-gather.13.cloned.1.call-done, f32[2,384]{1,0:T(2,128)S(1)} %add_multiply_fusion.1), kind=kOutput, calls=%fused_computation.14 | convolution fusion | flops 6644588544 | bytes 18189312 | tf_op jit(solution)/shard_map/nd,mdf->mnf/dot_general | solution.py:231
  274.6 1.4 fusion.24
  276.0 17.5 %all-to-all-done.1 = bf16[64,16,1536]{2,1,0:T(8,128)(2,1)S(1)} async-done(((bf16[64,16,1536]{2,1,0:T(8,128)(2,1)}), bf16[64,16,1536]{2,1,0:T(8,128)(2,1)S(1)}, u32[]{:S(2)}, u32[]{:S(2)}) %all-to-all-start.1) | async-done | bytes 3145760 | tf_op jit(solution)/shard_map/all_to_all | solution.py:191
  293.5 0.7 abs_reduce_fusion.1
  294.2 0.9 copy-done
  295.2 1.0 slice.155
  296.4 1.0 copy.30
  297.4 1.1 reshape.299
  298.9 1.1 select_add_fusion.mixing
  300.0 16.7 %all-gather.9.cloned.1.call-done = bf16[4,1056,384]{2,1,0:T(8,128)(2,1)} async-done(((bf16[1,1056,384]{2,1,0:T(8,128)(2,1)}), bf16[4,1056,384]{2,1,0:T(8,128)(2,1)}) %all-gather.9.cloned.1.call-update) | async-done | bytes 3244048 | tf_op jit(solution)/shard_map/all_gather | solution.py:234
  316.7 2.3 slice_bitcast_fusion.3
  319.6 3.7 fusion.12
  323.3 55.0 %give_back.1 = (bf16[16,4096]{1,0:T(8,128)(2,1)S(1)}, f32[8,8,16,128]{3,2,1,0:T(8,128)S(1)}) custom-call(bf16[4,264,1024]{2,1,0:T(8,128)(2,1)S(1)} %bitcast.81, f32[2,256,512]{2,1,0:T(8,128)S(1)} %select_add_fusion.mixing, f32[16,128]{1,0:T(8,128)S(1)} %maximum_bitcast_fusion.1.scales), custom_call_target="tpu_custom_call" | custom-call | flops 20000000000 | bytes 10000000 | tf_op jit(solution)/shard_map/give_back/pallas_call | solution.py:132
  379.1 0.7 dynamic-slice.1
  (57 shorter events, 4.3 us)
Async XLA Ops:
  7.2 41.8 %all-gather.7.cloned.1.call-start = ((), (), s32[]{:S(2)}) async-start(), calls=%async_computation.2 | async-start | bytes 1216512 | tf_op jit(solution)/shard_map/all_gather | solution.py:187
  11.6 134.5 %all-gather.11.cloned.1.call-start = ((), (), s32[]{:S(2)}) async-start(), calls=%async_computation.4 | async-start | bytes 9732096 | tf_op jit(solution)/shard_map/all_gather | solution.py:188
  56.0 159.9 %all-to-all-start = ((bf16[256,2,16,384]{3,2,1,0:T(8,128)(2,1)}), bf16[256,2,16,384]{3,2,1,0:T(8,128)(2,1)}, u32[]{:S(2)}, u32[]{:S(2)}) async-start(bf16[256,2,16,384]{3,2,1,0:T(8,128)(2,1)} %pad_maximum_fusion), calls=%async_computation | async-start | bytes 12582912 | tf_op jit(solution)/shard_map/all_to_all | solution.py:190
  72.3 191.1 %all-gather.13.cloned.1.call-start = ((), (), s32[]{:S(2)}) async-start(), calls=%async_computation.5 | async-start | bytes 10813440 | tf_op jit(solution)/shard_map/all_gather | solution.py:209
  157.1 63.2 %copy-start.2 = (s32[64]{0:T(128)S(1)}, s32[64]{0:T(128)}, u32[]{:S(2)}) copy-start(s32[64]{0:T(128)} %param.9) | copy-start | bytes 772
  215.9 77.6 %all-to-all-start.1 = ((bf16[64,16,1536]{2,1,0:T(8,128)(2,1)}), bf16[64,16,1536]{2,1,0:T(8,128)(2,1)S(1)}, u32[]{:S(2)}, u32[]{:S(2)}) async-start(bf16[64,16,1536]{2,1,0:T(8,128)(2,1)} %bitcast.84), calls=%async_computation.1 | async-start | bytes 6291456 | tf_op jit(solution)/shard_map/all_to_all | solution.py:191
  220.2 96.5 %all-gather.9.cloned.1.call-start = ((), (), s32[]{:S(2)}) async-start(), calls=%async_computation.3 | async-start | bytes 4055040 | tf_op jit(solution)/shard_map/all_gather | solution.py:234
  293.5 1.7 copy-start
  316.7 2.9 copy-start.1
Sparse Core Ops, SparseCore 0:
  11.7 37.2 all-gather.6
  50.9 95.1 all-gather.10
  157.3 106.0 all-gather.12
  276.1 40.5 all-gather.8
